TPU v7x, 32 devices: a whole 2x2x4 slice. The times are simulated.
32 devices in a mesh: seq: 8 (over z, y), grp: 4 (over x, core).
Axes of the slice: x: 2, y: 2, z: 4, core: 2. Of those that a mesh axis runs over, the one named last changes fastest.
Arguments:
- query_nope: bfloat16 [4, 2, 128, 128], P(None, None, 'seq'), may hold values from -12.859821 to 12.859821
- query_rope: bfloat16 [4, 2, 128, 64], P(None, None, 'seq'), may hold values from -150 to 150
- latent_cache: bfloat16 [4, 8192, 576], P(None, ('seq', 'grp')), may hold values from -5 to 5
- lengths: int32 [4], replicated, may hold values from 4096 to 8192
- key_weight: bfloat16 [128, 128, 512], P('seq'), may hold values from -0.5 to 0.5
- value_weight: bfloat16 [128, 512, 128], P('seq'), may hold values from -0.25 to 0.25
- output_weight: bfloat16 [16384, 7168], P('seq', 'grp'), may hold values from -0.0625 to 0.0625
Outputs:
- mixed: bfloat16 [4, 2, 7168], P(None, None, ('grp', 'seq'))
All inputs are finite; a program needn't handle non-finite values.
Results may differ from a plain program's by a relative error of at most 0.0095.
Values may be sent and summed in bfloat16 or wider, within the bound.
No kernel may reach another device: no remote copies, remote signals or barrier semaphores. Data moves between devices by JAX's collectives and lax.ppermute only.
A program may use at most 64 MiB of HBM per device.

v0:
```python
import jax
import jax.numpy as jnp
from jax import lax
from jax.sharding import PartitionSpec as P

NEGATIVE = -1e30


def joined(part, axis, combine):
    gathered = jax.tree.map(lambda a: lax.all_gather(a, axis), part)

    def take(source):
        return jax.tree.map(lambda a: lax.dynamic_index_in_dim(a, source, 0, False), gathered)

    return lax.fori_loop(
        1, lax.axis_size(axis), lambda source, state: combine(state, take(source)), take(0)
    )


def shard_partial(queries, cache_block, limits, offset, factor, latent_width):
    raw_score = (
        jnp.einsum("bqhd,bpd->bqhp", queries, cache_block, preferred_element_type=jnp.float32)
        * factor
    )
    places = offset + lax.broadcasted_iota(jnp.int32, (1, 1, cache_block.shape[1]), 2)
    visible = places < limits[:, :, None]
    scores = jnp.where(visible[:, :, None, :], raw_score, NEGATIVE)
    maxima = jnp.max(scores, axis=-1)
    powers = jnp.exp(scores - maxima[..., None])
    totals = jnp.sum(powers, axis=-1)
    weights = powers.astype(jnp.bfloat16)
    summed = jnp.einsum(
        "bqhp,bpd->bqhd",
        weights,
        cache_block[:, :, :latent_width],
        preferred_element_type=jnp.float32,
    )
    return (maxima, totals, (summed / totals[..., None]).astype(jnp.bfloat16))


def merge_sources(partials, maxima, totals):
    highest = jnp.max(maxima, axis=0)
    shares = totals * jnp.exp(maxima - highest[None])
    summed = jnp.sum(shares, axis=0)
    numerator = jnp.sum(shares[..., None] * partials.astype(jnp.float32), axis=0)
    return (highest, summed, numerator / summed[..., None])


def merge_tuple(received):
    return merge_sources(received[0], received[1], received[2])


def join_pairs(earlier, later):
    highest = jnp.maximum(earlier[0], later[0])
    left_share = earlier[1] * jnp.exp(earlier[0] - highest)
    right_share = later[1] * jnp.exp(later[0] - highest)
    summed = left_share + right_share
    blended = (left_share[..., None] * earlier[2] + right_share[..., None] * later[2]) / summed[
        ..., None
    ]
    return (highest, summed, blended)


def absorb(query_nope, query_rope, key_weight):
    absorbed = jnp.einsum(
        "bqhn,hnd->bqhd", query_nope, key_weight, preferred_element_type=jnp.float32
    )
    return jnp.concatenate([absorbed.astype(jnp.bfloat16), query_rope], axis=-1)


def up_project(latent_out, value_weight):
    values = jnp.einsum(
        "bqhd,hde->bqhe", latent_out, value_weight, preferred_element_type=jnp.float32
    ).astype(jnp.bfloat16)
    return values.reshape(values.shape[0], values.shape[1], values.shape[2] * values.shape[3])


def shards(query_nope, query_rope, latent_cache, lengths, key_weight, value_weight, output_weight):
    latent_width = key_weight.shape[2]
    factor = float(query_nope.shape[3] + query_rope.shape[3]) ** (-0.5)
    positions = latent_cache.shape[1]
    drafts = query_nope.shape[1]
    offset = (lax.axis_index("seq") * lax.axis_size("grp") + lax.axis_index("grp")) * positions
    limits = lengths[:, None] - drafts + 1 + lax.broadcasted_iota(jnp.int32, (1, drafts), 1)
    own_queries = absorb(query_nope, query_rope, key_weight)
    maxima, totals, partials = shard_partial(
        lax.all_gather(own_queries, "seq", axis=2, tiled=True),
        latent_cache,
        limits,
        offset,
        factor,
        latent_width,
    )
    partials, maxima, totals = (partials, maxima, totals)
    sources = (partials[None], maxima[None], totals[None])
    gathered = merge_tuple(
        (
            lax.all_to_all(
                sources[0].astype(jnp.float32), "seq", split_axis=3, concat_axis=0, tiled=True
            ).astype(jnp.bfloat16),
            lax.all_to_all(sources[1], "seq", split_axis=3, concat_axis=0, tiled=True),
            lax.all_to_all(sources[2], "seq", split_axis=3, concat_axis=0, tiled=True),
        )
    )
    highest, summed, blended = joined((gathered[0], gathered[1], gathered[2]), "grp", join_pairs)
    values = up_project(blended.astype(jnp.bfloat16), value_weight)
    head_terms = jnp.dot(values, output_weight, preferred_element_type=jnp.float32)
    reduced = lax.psum_scatter(head_terms, "seq", scatter_dimension=2, tiled=True)
    return reduced.astype(jnp.bfloat16)


def solution(mesh):
    in_specs = (
        P(None, None, "seq", None),
        P(None, None, "seq", None),
        P(None, ("seq", "grp"), None),
        P(),
        P("seq", None, None),
        P("seq", None, None),
        P("seq", "grp"),
    )
    out_specs = P(None, None, ("grp", "seq"))
    return jax.shard_map(shards, mesh=mesh, in_specs=in_specs, out_specs=out_specs, check_vma=False)
```

profile of v0, /device:TPU:0, one launch (start us, length us, event | category | flops | bytes accessed | tf_op | source)
XLA Modules:
  0.0 212.3 jit_solution(17703678175560071938)
XLA Ops:
  6.5 0.9 copy.29
  7.5 0.7 copy-done
  8.1 1.1 fusion.18
  9.3 0.8 pad_maximum_fusion
  10.2 44.5 %all-gather.5.cloned.1.call-done = bf16[4,2,128,576]{3,0,1,2:T(4,128)(2,1)} async-done(((bf16[4,2,16,576]{3,0,1,2:T(4,128)(2,1)}), bf16[4,2,128,576]{3,0,1,2:T(4,128)(2,1)}) %all-gather.5.cloned.1.call-update) | async-done | bytes 1179664 | tf_op jit(solution)/shard_map/all_gather | solution.py:87
  54.7 2.4 %fusion.42 = (f32[4,2,128]{2,1,0:T(2,128)S(1)}, f32[4,2,128,256]{3,2,1,0:T(8,128)S(1)}) fusion(bf16[4,256,576]{1,2,0:T(8,128)(2,1)} %param.11, bf16[4,2,128,576]{3,0,1,2:T(4,128)(2,1)} %all-gather.5.cloned.1.call-done, pred[4,2,256]{2,1,0:T(4,128)(4,1)S(1)} %broadcast_compare_fusion), kind=kOutput, calls=%fused_computation.50 | convolution fusion | flops 302775296 | bytes 3414016 | tf_op jit(solution)/shard_map/bqhd,bpd->bqhp/dot_general | solution.py:22
  57.1 0.4 fusion.30
  57.5 0.2 copy.34
  57.7 0.8 reshape.85
  58.5 3.4 %all-to-all-start.1 = ((f32[8,1,128]{2,1,0:T(1,128)}), f32[8,1,128]{2,1,0:T(1,128)S(1)}, u32[]{:S(2)}, u32[]{:S(2)}) async-start(f32[8,1,128]{2,1,0:T(1,128)} %reshape.85), calls=%async_computation.1 | async-start | bytes 8192 | tf_op jit(solution)/shard_map/all_to_all | solution.py:102
  61.9 0.2 copy.31
  62.1 0.8 reshape.83
  62.9 5.5 %all-to-all-done.1 = f32[8,1,128]{2,1,0:T(1,128)S(1)} async-done(((f32[8,1,128]{2,1,0:T(1,128)}), f32[8,1,128]{2,1,0:T(1,128)S(1)}, u32[]{:S(2)}, u32[]{:S(2)}) %all-to-all-start.1) | async-done | bytes 4128 | tf_op jit(solution)/shard_map/all_to_all | solution.py:102
  68.4 3.3 %all-to-all-start = ((f32[8,1,128]{2,1,0:T(1,128)}), f32[8,1,128]{2,1,0:T(1,128)S(1)}, u32[]{:S(2)}, u32[]{:S(2)}) async-start(f32[8,1,128]{2,1,0:T(1,128)} %reshape.83), calls=%async_computation | async-start | bytes 8192 | tf_op jit(solution)/shard_map/all_to_all | solution.py:101
  71.7 1.7 fusion.11
  73.5 2.1 copy.38
  75.6 2.5 %all-to-all-done = f32[8,1,128]{2,1,0:T(1,128)S(1)} async-done(((f32[8,1,128]{2,1,0:T(1,128)}), f32[8,1,128]{2,1,0:T(1,128)S(1)}, u32[]{:S(2)}, u32[]{:S(2)}) %all-to-all-start) | async-done | bytes 4128 | tf_op jit(solution)/shard_map/all_to_all | solution.py:101
  78.1 3.6 %all-to-all-start.2 = ((bf16[1,4,2,128,512]{4,2,1,0,3:T(2,128)(2,1)}), bf16[1,4,2,128,512]{4,2,1,0,3:T(2,128)(2,1)S(1)}, u32[]{:S(2)}, u32[]{:S(2)}) async-start(bf16[1,4,2,128,512]{4,2,1,0,3:T(2,128)(2,1)} %copy.38), calls=%async_computation.2 | async-start | bytes 2097152 | tf_op jit(solution)/shard_map/all_to_all | solution.py:98
  81.7 0.5 broadcast.51
  82.2 0.7 reduce.2
  82.9 0.2 reshape.86
  83.1 1.6 copy.35
  84.7 0.7 reduce.1
  85.4 0.2 reshape.84
  85.6 0.9 copy.32
  86.6 1.8 fusion.40
  88.4 16.5 %all-to-all-done.2 = bf16[1,4,2,128,512]{4,2,1,0,3:T(2,128)(2,1)S(1)} async-done(((bf16[1,4,2,128,512]{4,2,1,0,3:T(2,128)(2,1)}), bf16[1,4,2,128,512]{4,2,1,0,3:T(2,128)(2,1)S(1)}, u32[]{:S(2)}, u32[]{:S(2)}) %all-to-all-start.2) | async-done | bytes 1048608 | tf_op jit(solution)/shard_map/all_to_all | solution.py:98
  104.9 2.3 %fusion.7 = f32[4,2,16,512]{3,1,0,2:T(2,128)S(1)} fusion(bf16[1,4,2,8,16,512]{5,2,1,4,3,0:T(2,128)(2,1)S(1)} %bitcast.108, f32[8,4,2,16]{2,1,3,0:T(4,128)} %get-tuple-element.201), kind=kLoop, calls=%fused_computation.13 | loop fusion | flops 1507328 | bytes 1314816 | tf_op jit(solution)/shard_map/reduce_sum | solution.py:45
  107.2 0.2 bitcast_divide_fusion
  107.3 0.9 copy.39
  108.3 0.1 copy.33
  108.4 0.1 copy.36
  108.5 5.2 %all-gather.1 = f32[16,2,16]{2,1,0:T(2,128)S(1)} all-gather(f32[4,2,16]{2,1,0:T(2,128)S(1)} %copy.36), channel_id=3, replica_groups=mesh['seq'=8,'grp'=4] {'grp'}, dimensions={0}, use_global_device_ids=true | all-gather | bytes 2560 | tf_op jit(solution)/shard_map/all_gather | solution.py:10
  113.7 5.2 %all-gather = f32[16,2,16]{2,1,0:T(2,128)S(1)} all-gather(f32[4,2,16]{2,1,0:T(2,128)S(1)} %copy.33), channel_id=2, replica_groups=mesh['seq'=8,'grp'=4] {'grp'}, dimensions={0}, use_global_device_ids=true | all-gather | bytes 2560 | tf_op jit(solution)/shard_map/all_gather | solution.py:10
  118.9 5.1 %all-gather.7.cloned.1.call-done = f32[4,4,2,16,512]{4,3,2,1,0:T(8,128)} async-done(((f32[1,4,2,16,512]{4,3,2,1,0:T(8,128)}), f32[4,4,2,16,512]{4,3,2,1,0:T(8,128)}) %all-gather.7.cloned.1.call-update) | async-done | bytes 1048592 | tf_op jit(solution)/shard_map/all_gather | solution.py:10
  124.0 1.0 slice_bitcast_fusion
  124.9 3.5 %while.19 = (s32[]{:T(128)}, f32[4,2,16]{2,1,0:T(2,128)S(1)}, f32[4,2,16]{2,1,0:T(2,128)S(1)}, f32[4,2,16,512]{3,2,1,0:T(8,128)S(1)}, f32[4,4,2,16]{3,2,1,0:T(2,...) while((s32[]{:T(128)}, f32[4,2,16]{2,1,0:T(2,128)S(1)}, ...), condition=%wide.region_6.7_spmd, body=%wide.region_5.6_spmd.sunk | while | flops 262917 | bytes 792207 | solution.py:15
  125.0 1.1 fusion.46
  126.2 1.1 fusion.46
  127.3 1.1 fusion.46
  128.4 2.0 fusion.24
  130.5 4.2 %fusion.3 = f32[4,2,1792]{2,0,1:T(4,128)S(1)} fusion(bf16[2048,1792]{1,0:T(8,128)(2,1)} %param.15, bf16[16,2,1,4,128]{4,3,2,1,0:T(4,128)(2,1)S(1)} %fusion.24), kind=kOutput, calls=%fused_computation.8 | convolution fusion | flops 58720256 | bytes 7430144 | tf_op jit(solution)/shard_map/dot_general | solution.py:107
  134.7 2.3 %copy.49 = f32[4,2,1792]{0,1,2:T(2,128)} copy(f32[4,2,1792]{2,0,1:T(4,128)S(1)} %fusion.3) | data formatting | bytes 114688
  137.0 3.1 %reshape.81 = f32[1792,8]{1,0:T(8,128)} reshape(f32[1792,2,4]{2,1,0:T(2,128)} %bitcast.107) | data formatting | bytes 114688
  140.1 63.9 %reduce-scatter.4.cloned.1.call-done = f32[224,8]{1,0:T(8,128)} async-done(((f32[1792,8]{1,0:T(8,128)}), f32[224,8]{1,0:T(8,128)}) %reduce-scatter.4.cloned.1.call-update) | async-done | bytes 7184
  204.0 1.0 reshape.82
  205.0 0.1 copy.50
  205.1 0.6 copy.43
  (20 shorter events, 0.5 us)
Async XLA Ops:
  6.5 1.6 copy-start
  6.5 3.5 %copy-start.1 = (s32[4]{0:T(128)S(1)}, s32[4]{0:T(128)}, u32[]{:S(2)}) copy-start(s32[4]{0:T(128)} %param.12) | copy-start | bytes 52
  6.5 48.2 %all-gather.5.cloned.1.call-start = ((), (), s32[]{:S(2)}) async-start(), calls=%async_computation.4 | async-start | bytes 1474560 | tf_op jit(solution)/shard_map/all_gather | solution.py:87
  58.5 9.9 %all-to-all-start.1 = ((f32[8,1,128]{2,1,0:T(1,128)}), f32[8,1,128]{2,1,0:T(1,128)S(1)}, u32[]{:S(2)}, u32[]{:S(2)}) async-start(f32[8,1,128]{2,1,0:T(1,128)} %reshape.85), calls=%async_computation.1 | async-start | bytes 8192 | tf_op jit(solution)/shard_map/all_to_all | solution.py:102
  68.4 9.7 %all-to-all-start = ((f32[8,1,128]{2,1,0:T(1,128)}), f32[8,1,128]{2,1,0:T(1,128)S(1)}, u32[]{:S(2)}, u32[]{:S(2)}) async-start(f32[8,1,128]{2,1,0:T(1,128)} %reshape.83), calls=%async_computation | async-start | bytes 8192 | tf_op jit(solution)/shard_map/all_to_all | solution.py:101
  78.1 26.8 %all-to-all-start.2 = ((bf16[1,4,2,128,512]{4,2,1,0,3:T(2,128)(2,1)}), bf16[1,4,2,128,512]{4,2,1,0,3:T(2,128)(2,1)S(1)}, u32[]{:S(2)}, u32[]{:S(2)}) async-start(bf16[1,4,2,128,512]{4,2,1,0,3:T(2,128)(2,1)} %copy.38), calls=%async_computation.2 | async-start | bytes 2097152 | tf_op jit(solution)/shard_map/all_to_all | solution.py:98
  81.6 42.3 %all-gather.7.cloned.1.call-start = ((), (), s32[]{:S(2)}) async-start(), calls=%async_computation.5 | async-start | bytes 1310720 | tf_op jit(solution)/shard_map/all_gather | solution.py:10
  108.2 95.8 %reduce-scatter.4.cloned.1.call-start = ((), (), s32[]{:S(2)}) async-start(), calls=%async_computation.6 | async-start | bytes 1032192
Sparse Core Ops, SparseCore 0:
  10.2 44.5 all-gather.4
  108.4 15.5 all-gather.6
  140.3 63.6 reduce-scatter.3
where the time goes:
time: 213 us; the launch traced here: 212 us
  waiting for transfers between devices  138 us (65%)
  local copies, waits for them, and re-layouts  18.2 us (9%)
  between operations  13.3 us (6%)
  matrix products  11.5 us (5%)
  starting transfers between devices  10.4 us (5%)
  blocking collectives  10.4 us (5%)
  other arithmetic  10.3 us (5%)
    unnamed x4, waiting for transfers between devices  63.9 us
    all_gather x1, waiting for transfers between devices, shards(): lax.all_gather(own_queries, 'seq', axis=2, tiled=True)  44.5 us
    all_to_all x1, waiting for transfers between devices, shards(): lax.all_to_all(sources[0].astype(jnp.float32), 'seq', split_axis=3, conca...  16.5 us
    all_gather x2, blocking collectives, joined(): gathered = jax.tree.map(lambda a: lax.all_gather(a, axis), part)  10.4 us
    unnamed x13, local copies, waits for them, and re-layouts  10.2 us
    all_to_all x1, waiting for transfers between devices, shards(): lax.all_to_all(sources[2], 'seq', split_axis=3, concat_axis=0, tiled=True)  5.53 us
    all_gather x1, waiting for transfers between devices, joined(): gathered = jax.tree.map(lambda a: lax.all_gather(a, axis), part)  5.1 us
  transfers between devices with their start and end apart: 6, of which 6 were waited for; matrix products, arithmetic and copies ran while one was open for 6% of the time, Pallas kernels for 0%

commit v1 on v0

v1 whole, which is shorter than its diff:
```python
import functools

import jax
import jax.numpy as jnp
from jax import lax
from jax.experimental import pallas as pl
from jax.experimental.pallas import tpu as pltpu
from jax.sharding import PartitionSpec as P

NEGATIVE = -1e30
LANES = 128


def split3(x):
    high = x.astype(jnp.bfloat16).astype(jnp.float32)
    rest = x - high
    middle = rest.astype(jnp.bfloat16).astype(jnp.float32)
    return high, middle, rest - middle


def attention_kernel(
    factor, latent, heads, offsets, limits, query, *refs
):
    caches, out = refs[:-1], refs[-1]
    rows = query.shape[0]
    width = caches[0].shape[1]
    drafts = limits.shape[0]
    token = (lax.broadcasted_iota(jnp.int32, (rows, 1), 0) // heads) % drafts
    limit = jnp.full((rows, 1), limits[0], jnp.int32)
    for t in range(1, drafts):
        limit = jnp.where(token == t, limits[t], limit)
    queries = query[...]
    scores = []
    for j, cache in enumerate(caches):
        raw = jnp.dot(queries, cache[...], preferred_element_type=jnp.float32) * factor
        places = offsets[j] + lax.broadcasted_iota(jnp.int32, (rows, width), 1)
        scores.append(jnp.where(places < limit, raw, NEGATIVE))
    top = functools.reduce(jnp.maximum, scores).max(axis=-1, keepdims=True)
    total = jnp.zeros((rows, 1), jnp.float32)
    summed = jnp.zeros((rows, latent), jnp.float32)
    for j, cache in enumerate(caches):
        expo = jnp.exp(scores[j] - top)
        total = total + jnp.sum(expo, axis=-1, keepdims=True)
        summed = summed + lax.dot_general(
            expo.astype(jnp.bfloat16),
            cache[:latent, :],
            (((1,), (1,)), ((), ())),
            preferred_element_type=jnp.float32,
        )
    out[:, :latent] = (summed / total).astype(jnp.bfloat16)
    lane = lax.broadcasted_iota(jnp.int32, (rows, LANES), 1)
    packed = jnp.zeros((rows, LANES), jnp.float32)
    for i, piece in enumerate(split3(top) + split3(total)):
        packed = jnp.where(lane == i, piece, packed)
    out[:, latent:] = packed.astype(jnp.bfloat16)


def merge_kernel(latent, received, out):
    block = received[...].astype(jnp.float32)
    stats = block[:, :, latent:]
    top = (stats[:, :, 0:1] + stats[:, :, 1:2]) + stats[:, :, 2:3]
    total = (stats[:, :, 3:4] + stats[:, :, 4:5]) + stats[:, :, 5:6]
    peak = jnp.max(top, axis=0, keepdims=True)
    share = total * jnp.exp(top - peak)
    numerator = jnp.sum(share * block[:, :, :latent], axis=0)
    out[...] = (numerator / jnp.sum(share, axis=0)).astype(jnp.bfloat16)


def whole(count):
    return [pl.BlockSpec(memory_space=pltpu.VMEM)] * count


def shards(query_nope, query_rope, latent_cache, lengths, key_weight, value_weight, output_weight):
    n_seq, n_grp = lax.axis_size("seq"), lax.axis_size("grp")
    seq, grp = lax.axis_index("seq"), lax.axis_index("grp")
    requests, drafts, heads, nope = query_nope.shape
    latent = key_weight.shape[2]
    positions, width = latent_cache.shape[1:]
    factor = float(nope + query_rope.shape[3]) ** (-0.5)
    assert requests == n_grp

    by_width = jnp.swapaxes(latent_cache, 1, 2)

    def request(array, index):
        return lax.dynamic_index_in_dim(array, index, 0, False)

    def partner(k):
        if n_grp & (n_grp - 1) == 0:
            return lambda i: i ^ k
        return lambda i: (k - i) % n_grp

    steps = range(n_grp)
    caches, holders = [], []
    for k in steps:
        other = partner(k)
        piece = request(by_width, other(grp))
        if k or other(1) != 1:
            piece = lax.ppermute(piece, "grp", [(i, other(i)) for i in range(n_grp)])
        caches.append(piece)
        holders.append(other(grp))
    offsets = jnp.stack([(seq * n_grp + holder) * positions for holder in holders])
    limits = request(lengths, grp) - drafts + 1 + jnp.arange(drafts, dtype=jnp.int32)

    absorbed = jnp.einsum(
        "qhn,hnd->qhd", request(query_nope, grp), key_weight, preferred_element_type=jnp.float32
    ).astype(jnp.bfloat16)
    own = jnp.concatenate([absorbed, request(query_rope, grp)], axis=-1)
    own = own.reshape(1, drafts * heads, width)
    queries = lax.all_to_all(
        jnp.broadcast_to(own, (n_seq,) + own.shape[1:]), "seq", 0, 0, tiled=True
    ).reshape(n_seq * drafts * heads, width)

    rows = n_seq * drafts * heads
    partial = pl.pallas_call(
        functools.partial(attention_kernel, factor, latent, heads),
        out_shape=jax.ShapeDtypeStruct((rows, latent + LANES), jnp.bfloat16),
        in_specs=[pl.BlockSpec(memory_space=pltpu.SMEM)] * 2 + whole(1 + n_grp),
        out_specs=pl.BlockSpec(memory_space=pltpu.VMEM),
        compiler_params=pltpu.CompilerParams(vmem_limit_bytes=12 << 20),
        name="attention",
    )(offsets, limits, queries, *caches)

    received = lax.all_to_all(
        partial.reshape(n_seq, drafts * heads, latent + LANES), "seq", 0, 0, tiled=True
    )
    latent_out = pl.pallas_call(
        functools.partial(merge_kernel, latent),
        out_shape=jax.ShapeDtypeStruct((drafts * heads, latent), jnp.bfloat16),
        in_specs=whole(1),
        out_specs=pl.BlockSpec(memory_space=pltpu.VMEM),
        compiler_params=pltpu.CompilerParams(vmem_limit_bytes=4 << 20),
        name="merge",
    )(received)

    values = jnp.einsum(
        "qhd,hde->qhe",
        latent_out.reshape(drafts, heads, latent),
        value_weight,
        preferred_element_type=jnp.float32,
    ).astype(jnp.bfloat16)
    values = lax.all_gather(values.reshape(drafts, -1), "grp", axis=0, tiled=True)
    terms = jnp.dot(values, output_weight, preferred_element_type=jnp.float32)
    tokens, columns = terms.shape
    terms = terms.reshape(tokens, n_seq, columns // n_seq).swapaxes(0, 1)
    terms = lax.all_to_all(terms, "seq", 0, 0, tiled=True)
    mixed = jnp.sum(terms, axis=0).astype(jnp.bfloat16)
    return mixed.reshape(requests, drafts, columns // n_seq)


def solution(mesh):
    in_specs = (
        P(None, None, "seq", None),
        P(None, None, "seq", None),
        P(None, ("seq", "grp"), None),
        P(),
        P("seq", None, None),
        P("seq", None, None),
        P("seq", "grp"),
    )
    out_specs = P(None, None, ("grp", "seq"))
    return jax.shard_map(shards, mesh=mesh, in_specs=in_specs, out_specs=out_specs, check_vma=False)
```

time: 213 us -> 68.3 us (0.32)
  waiting for transfers between devices: 138 us -> 12.5 us
  blocking collectives: 10.4 us -> 31.8 us
  between operations: 13.3 us -> 0.7 us
  local copies, waits for them, and re-layouts: 18.2 us -> 5.94 us
  other arithmetic: 10.3 us -> 0.1 us
  matrix products: 11.5 us -> 4.89 us
  Pallas kernels: 0 us -> 2.49 us
    unnamed x4 -> x0, waiting for transfers between devices: 63.9 us -> none
    all_gather x2 -> x0, waiting for transfers between devices: 49.6 us -> none  [the longest x1 44.5 us: shards(): lax.all_gather(own_queries, 'seq', axis=2, tiled=True)]
    all_to_all x0 -> x2, blocking collectives: none -> 26.6 us  [the longest x1 16.9 us: shards(): lax.all_to_all(partial.reshape(n_seq, drafts * heads, latent + LANES), 's...]
    all_to_all x3 -> x1, waiting for transfers between devices: 24.6 us -> 0.01 us  [shards(): lax.all_to_all(jnp.broadcast_to(own, (n_seq,) + own.shape[1:]), 'seq', 0,...]
    ppermute x0 -> x3, waiting for transfers between devices: none -> 12.5 us  [shards(): piece = lax.ppermute(piece, 'grp', [(i, other(i)) for i in range(n_grp)])]
    unnamed x13 -> x7, local copies, waits for them, and re-layouts: 10.2 us -> 0.09 us
    dot_general x5 -> x3, matrix products: 11.5 us -> 4.89 us  [the longest x1 4.14 us: shards(): terms = jnp.dot(values, output_weight, preferred_element_type=jnp.float32)]
    all_gather x2 -> x1, blocking collectives: 10.4 us -> 5.19 us  [shards(): lax.all_gather(values.reshape(drafts, -1), 'grp', axis=0, tiled=True)]
  transfers between devices with their start and end apart: 6 -> 4, of which waited for: 6 -> 2; matrix products, arithmetic and copies ran while one was open for 6% -> 4% of each run, Pallas kernels for 0% -> 0%
where the time goes in v1:
time: 68.3 us; the launch traced here: 67.9 us
  blocking collectives  31.8 us (47%)
  waiting for transfers between devices  12.5 us (18%)
  starting transfers between devices  9.45 us (14%)
  local copies, waits for them, and re-layouts  5.94 us (9%)
  matrix products  4.89 us (7%)
  Pallas kernels  2.49 us (4%)
  between operations  0.7 us (1%)
    all_to_all x1, blocking collectives, shards(): lax.all_to_all(partial.reshape(n_seq, drafts * heads, latent + LANES), 's...  16.9 us
    ppermute x3, waiting for transfers between devices, shards(): piece = lax.ppermute(piece, 'grp', [(i, other(i)) for i in range(n_grp)])  12.5 us
    all_to_all x1, blocking collectives, shards(): terms = lax.all_to_all(terms, 'seq', 0, 0, tiled=True)  9.7 us
    all_to_all x1, starting transfers between devices, shards(): lax.all_to_all(jnp.broadcast_to(own, (n_seq,) + own.shape[1:]), 'seq', 0,...  7.31 us
    all_gather x1, blocking collectives, shards(): lax.all_gather(values.reshape(drafts, -1), 'grp', axis=0, tiled=True)  5.19 us
    dot_general x1, matrix products, shards(): terms = jnp.dot(values, output_weight, preferred_element_type=jnp.float32)  4.14 us
    squeeze x1, local copies, waits for them, and re-layouts, request(): return lax.dynamic_index_in_dim(array, index, 0, False)  2.2 us
    pallas_call x1, Pallas kernels, shards(): pl.pallas_call(functools.partial(attention_kernel, factor, latent, heads)...  2.19 us
  transfers between devices with their start and end apart: 4, of which 2 were waited for; matrix products, arithmetic and copies ran while one was open for 4% of the time, Pallas kernels for 0%

profile of v1, /device:TPU:0, one launch (start us, length us, event | category | flops | bytes accessed | tf_op | source)
XLA Modules:
  0.0 67.9 jit_solution(15832131251319304393)
XLA Ops:
  0.0 0.0 copy-start
  0.0 0.8 %constant_dynamic-slice_fusion.1 = bf16[1,2,16,128]{3,2,1,0:T(8,128)(2,1)S(1)} fusion(bf16[4,2,16,128]{3,2,1,0:T(8,128)(2,1)} %param.7, s32[]{:T(128)S(6)} %select_n.19), kind=kLoop, calls=%fused_computation.14 | loop fusion | bytes 16388 | tf_op jit(solution)/shard_map/jit(dynamic_index_in_dim)/dynamic_slice | solution.py:85
  0.9 0.7 %constant_dynamic-slice_fusion = bf16[1,2,16,64]{3,2,1,0:T(8,128)(2,1)S(1)} fusion(bf16[4,2,16,64]{3,2,1,0:T(8,128)(2,1)} %param.8, s32[]{:T(128)S(6)} %select_n.19), kind=kLoop, calls=%fused_computation.13 | loop fusion | bytes 8196 | tf_op jit(solution)/shard_map/jit(dynamic_index_in_dim)/dynamic_slice | solution.py:85
  1.5 0.1 copy-done
  1.6 0.4 fusion
  2.0 0.0 copy-start.2
  2.0 0.8 %broadcast_in_dim.8 = bf16[8,32,576]{2,1,0:T(8,128)(2,1)} broadcast(bf16[32,576]{1,0:T(8,128)(2,1)S(1)} %maximum_bitcast_fusion), dimensions={1,2} | broadcast | bytes 331776 | tf_op jit(solution)/shard_map/broadcast_in_dim | solution.py:110
  2.8 7.3 %all-to-all-start = ((bf16[8,32,576]{2,1,0:T(8,128)(2,1)}), bf16[8,32,576]{2,1,0:T(8,128)(2,1)S(1)}, u32[]{:S(2)}, u32[]{:S(2)}) async-start(bf16[8,32,576]{2,1,0:T(8,128)(2,1)} %broadcast_in_dim.8), calls=%async_computation | async-start | bytes 655360 | tf_op jit(solution)/shard_map/all_to_all | solution.py:109
  10.1 2.2 %dynamic-slice_bitcast_fusion = (bf16[576,256]{1,0:T(8,128)(2,1)}, bf16[576,256]{1,0:T(8,128)(2,1)}, bf16[576,256]{1,0:T(8,128)(2,1)S(1)}, bf16[576,256]{1,0:T(8,128)(2,1)}) fusion(bf16[4,256,576]{1,2,0:T(8,128)(2,1)} %param.9, s32[]{:T(128)S(6)} %select_n.22, s32[]{:T(128)S(6)} %select_n.20, s32[]{:T(128)S(6)} %select_n.19, s32[]{:T(128)S(6)} %select_n.21), kind=kLoop, calls=%fused_computation.4 | loop fusion | bytes 2359312 | tf_op jit(solution)/shard_map/jit(dynamic_index_in_dim)/squeeze | solution.py:85
  12.3 0.7 collective-permute-start.2
  13.0 1.0 %collective-permute-start = (bf16[576,256]{1,0:T(8,128)(2,1)}, bf16[576,256]{1,0:T(8,128)(2,1)S(1)}, u32[]{:S(2)}, u32[]{:S(2)}) collective-permute-start(bf16[576,256]{1,0:T(8,128)(2,1)} %get-tuple-element.6), channel_id=1, source_target_pairs={{0,1},{1,0},{2,3},{3,2},{4,5},{5,4},{6,7},{7,6},{8,9},{9,8},{10,11... | collective-permute-start | bytes 884744 | tf_op jit(solution)/shard_map/ppermute | solution.py:98
  13.9 0.5 collective-permute-start.1
  14.4 0.0 copy-done.2
  14.4 0.6 dynamic_slice.25
  15.7 0.1 pad_add_fusion.offsets
  15.8 6.0 %collective-permute-done.2.refs_3_ = bf16[576,256]{1,0:T(8,128)(2,1)S(1)} collective-permute-done((bf16[576,256]{1,0:T(8,128)(2,1)}, bf16[576,256]{1,0:T(8,128)(2,1)S(1)}, u32[]{:S(2)}, u32[]{:S(2)}) %collective-permute-start.2) | collective-permute-done | bytes 294944 | tf_op jit(solution)/shard_map/ppermute | solution.py:98
  21.8 0.0 collective-permute-done.refs_1_
  21.8 6.5 %collective-permute-done.1.refs_2_ = bf16[576,256]{1,0:T(8,128)(2,1)} collective-permute-done((bf16[576,256]{1,0:T(8,128)(2,1)}, bf16[576,256]{1,0:T(8,128)(2,1)}, u32[]{:S(2)}, u32[]{:S(2)}) %collective-permute-start.1) | collective-permute-done | bytes 294944 | tf_op jit(solution)/shard_map/ppermute | solution.py:98
  28.2 0.0 all-to-all-done
  28.2 0.0 copy-start.1
  28.2 2.2 %attention.1 = bf16[256,640]{1,0:T(8,128)(2,1)S(1)} custom-call(s32[4]{0:T(128)S(1)} %pad_add_fusion.offsets, s32[2]{0:T(128)S(1)} %iota_add_fusion.limits, bf16[256,576]{1,0:T(8,128)(2,1)S(1)} %bitcast.44, bf16[576,256]{1,0:T(8,128)(2,1)S(1)} %get-tuple-element.7.refs_0_, bf16[576,256]{1,0:T(8,128)(2,1)S(1)} %collective-permute-done.refs_1_, ...), custom_call_target="tpu_custom_call" | custom-call | tf_op jit(solution)/shard_map/attention/pallas_call | solution.py:114
  30.4 16.9 %all_to_all.15.received = bf16[8,32,640]{2,1,0:T(8,128)(2,1)S(1)} all-to-all(bf16[8,32,640]{2,1,0:T(8,128)(2,1)S(1)} %bitcast.45), channel_id=1, replica_groups=mesh['seq'=8,'grp'=4] {'seq'}, dimensions={0} | all-to-all | bytes 655360 | tf_op jit(solution)/shard_map/all_to_all | solution.py:123
  47.4 0.3 merge.1
  47.7 0.0 copy-done.1
  47.7 0.4 fusion.1
  48.1 5.2 %all-gather = bf16[4,2,2048]{2,1,0:T(2,128)(2,1)S(1)} all-gather(bf16[1,2,2048]{2,1,0:T(2,128)(2,1)S(1)} %fusion.1), channel_id=1, replica_groups=mesh['seq'=8,'grp'=4] {'grp'}, dimensions={0}, use_global_device_ids=true | all-gather | bytes 40960 | tf_op jit(solution)/shard_map/all_gather | solution.py:141
  53.3 4.1 %fusion.5 = f32[8,1792]{1,0:T(8,128)S(1)} fusion(bf16[8,2048]{1,0:T(8,128)(2,1)S(1)} %reshape.30, bf16[2048,1792]{1,0:T(8,128)(2,1)} %param.13), kind=kOutput, calls=%fused_computation.17 | convolution fusion | flops 58720256 | bytes 7430144 | tf_op jit(solution)/shard_map/dot_general | solution.py:142
  57.4 0.1 reshape.28
  57.6 9.7 %all_to_all.16 = f32[8,8,224]{2,1,0:T(8,128)S(1)} all-to-all(f32[8,8,224]{2,1,0:T(8,128)S(1)} %bitcast.47), channel_id=1, replica_groups=mesh['seq'=8,'grp'=4] {'seq'}, dimensions={0} | all-to-all | bytes 114688 | tf_op jit(solution)/shard_map/all_to_all | solution.py:145
  67.3 0.6 convert_element_type.24
  (6 shorter events, 0.1 us)
Async XLA Ops:
  0.0 1.6 %copy-start = (bf16[16,128,512]{2,1,0:T(8,128)(2,1)S(1)}, bf16[16,128,512]{2,1,0:T(8,128)(2,1)}, u32[]{:S(2)}) copy-start(bf16[16,128,512]{2,1,0:T(8,128)(2,1)} %param.11) | copy-start | bytes 6291460
  2.0 12.5 %copy-start.2 = (s32[4]{0:T(128)S(1)}, s32[4]{0:T(128)}, u32[]{:S(2)}) copy-start(s32[4]{0:T(128)} %param.10) | copy-start | bytes 52
  2.8 25.5 %all-to-all-start = ((bf16[8,32,576]{2,1,0:T(8,128)(2,1)}), bf16[8,32,576]{2,1,0:T(8,128)(2,1)S(1)}, u32[]{:S(2)}, u32[]{:S(2)}) async-start(bf16[8,32,576]{2,1,0:T(8,128)(2,1)} %broadcast_in_dim.8), calls=%async_computation | async-start | bytes 655360 | tf_op jit(solution)/shard_map/all_to_all | solution.py:109
  12.3 9.5 %collective-permute-start.2 = (bf16[576,256]{1,0:T(8,128)(2,1)}, bf16[576,256]{1,0:T(8,128)(2,1)S(1)}, u32[]{:S(2)}, u32[]{:S(2)}) collective-permute-start(bf16[576,256]{1,0:T(8,128)(2,1)} %get-tuple-element.5), channel_id=1, source_target_pairs={{0,3},{1,2},{2,1},{3,0},{4,7},{5,6},{6,5},{7,4},{8,11},{9,10},{10,... | collective-permute-start | bytes 884744 | tf_op jit(solution)/shard_map/ppermute | solution.py:98
  13.0 8.8 %collective-permute-start = (bf16[576,256]{1,0:T(8,128)(2,1)}, bf16[576,256]{1,0:T(8,128)(2,1)S(1)}, u32[]{:S(2)}, u32[]{:S(2)}) collective-permute-start(bf16[576,256]{1,0:T(8,128)(2,1)} %get-tuple-element.6), channel_id=1, source_target_pairs={{0,1},{1,0},{2,3},{3,2},{4,5},{5,4},{6,7},{7,6},{8,9},{9,8},{10,11... | collective-permute-start | bytes 884744 | tf_op jit(solution)/shard_map/ppermute | solution.py:98
  13.9 14.3 %collective-permute-start.1 = (bf16[576,256]{1,0:T(8,128)(2,1)}, bf16[576,256]{1,0:T(8,128)(2,1)}, u32[]{:S(2)}, u32[]{:S(2)}) collective-permute-start(bf16[576,256]{1,0:T(8,128)(2,1)} %get-tuple-element.8), channel_id=1, source_target_pairs={{0,2},{1,3},{2,0},{3,1},{4,6},{5,7},{6,4},{7,5},{8,10},{9,11},{10,... | collective-permute-start | bytes 884744 | tf_op jit(solution)/shard_map/ppermute | solution.py:98
  28.2 19.5 %copy-start.1 = (bf16[16,512,128]{2,1,0:T(8,128)(2,1)S(1)}, bf16[16,512,128]{2,1,0:T(8,128)(2,1)}, u32[]{:S(2)}) copy-start(bf16[16,512,128]{2,1,0:T(8,128)(2,1)} %param.12) | copy-start | bytes 6291460

commit v2 on v1

v2 whole, which is shorter than its diff:
```python
import functools

import jax
import jax.numpy as jnp
from jax import lax
from jax.experimental import pallas as pl
from jax.experimental.pallas import tpu as pltpu
from jax.sharding import PartitionSpec as P


NEGATIVE = -1e30
LANES = 128


def split3(x):
    high = x.astype(jnp.bfloat16).astype(jnp.float32)
    rest = x - high
    middle = rest.astype(jnp.bfloat16).astype(jnp.float32)
    return high, middle, rest - middle


def attention_kernel(factor, latent, heads, drafts, partners, lengths, query, *refs):
    caches, out = refs[:-1], refs[-1]
    rows = query.shape[0]
    width = caches[0].shape[1]
    seq, grp = lax.axis_index("seq"), lax.axis_index("grp")
    token = (lax.broadcasted_iota(jnp.int32, (rows, 1), 0) // heads) % drafts
    limit = lengths[grp] - drafts + 1 + token
    queries = query[...]
    scores = []
    for j, cache in enumerate(caches):
        raw = jnp.dot(queries, cache[...], preferred_element_type=jnp.float32) * factor
        offset = (seq * len(caches) + partners[j](grp)) * width
        places = offset + lax.broadcasted_iota(jnp.int32, (rows, width), 1)
        scores.append(jnp.where(places < limit, raw, NEGATIVE))
    top = functools.reduce(jnp.maximum, scores).max(axis=-1, keepdims=True)
    total = jnp.zeros((rows, 1), jnp.float32)
    summed = jnp.zeros((rows, latent), jnp.float32)
    for j, cache in enumerate(caches):
        expo = jnp.exp(scores[j] - top)
        total = total + jnp.sum(expo, axis=-1, keepdims=True)
        summed = summed + lax.dot_general(
            expo.astype(jnp.bfloat16),
            cache[:latent, :],
            (((1,), (1,)), ((), ())),
            preferred_element_type=jnp.float32,
        )
    out[:, :latent] = (summed / total).astype(jnp.bfloat16)
    lane = lax.broadcasted_iota(jnp.int32, (rows, LANES), 1)
    packed = jnp.zeros((rows, LANES), jnp.float32)
    for i, piece in enumerate(split3(top) + split3(total)):
        packed = jnp.where(lane == i, piece, packed)
    out[:, latent:] = packed.astype(jnp.bfloat16)


def stacked(array, heads):
    rows = array.shape[0]
    head = lax.broadcasted_iota(jnp.int32, (rows, 1), 0) % heads
    zero = jnp.zeros_like(array)
    return jnp.concatenate([jnp.where(head == h, array, zero) for h in range(heads)], axis=-1)


def pick_kernel(partners, cache, *refs):
    pieces, sems = refs[:-1], refs[-1]
    grp = lax.axis_index("grp")
    copies = [
        pltpu.make_async_copy(cache.at[partners[i](grp)], piece, sems.at[i])
        for i, piece in enumerate(pieces)
    ]
    for copy in copies:
        copy.start()
    for copy in copies:
        copy.wait()


def absorb_kernel(nope, rope, weight, queries, nope_block, rope_block, weights, sems):
    grp = lax.axis_index("grp")
    copies = [
        pltpu.make_async_copy(weight, weights, sems.at[0]),
        pltpu.make_async_copy(nope.at[grp], nope_block, sems.at[1]),
        pltpu.make_async_copy(rope.at[grp], rope_block, sems.at[2]),
    ]
    for copy in copies:
        copy.start()
    for copy in copies[::-1]:
        copy.wait()
    heads, depth, latent = weights.shape
    absorbed = jnp.dot(
        stacked(nope_block[...], heads),
        weights[...].reshape(heads * depth, latent),
        preferred_element_type=jnp.float32,
    ).astype(jnp.bfloat16)
    tail = rope_block[...]
    for i in range(queries.shape[0]):
        queries[i, :, :latent] = absorbed
        queries[i, :, latent:] = tail


def merge_kernel(latent, received, weight, out):
    block = received[...].astype(jnp.float32)
    stats = block[:, :, latent:]
    top = (stats[:, :, 0:1] + stats[:, :, 1:2]) + stats[:, :, 2:3]
    total = (stats[:, :, 3:4] + stats[:, :, 4:5]) + stats[:, :, 5:6]
    peak = jnp.max(top, axis=0, keepdims=True)
    share = total * jnp.exp(top - peak)
    numerator = jnp.sum(share * block[:, :, :latent], axis=0)
    merged = (numerator / jnp.sum(share, axis=0)).astype(jnp.bfloat16)
    heads, depth, width = weight.shape
    weights = weight[...].reshape(heads * depth, width)
    values = jnp.dot(stacked(merged, heads), weights, preferred_element_type=jnp.float32)
    out[...] = values.astype(jnp.bfloat16)


def project_kernel(values, weight, out, wide):
    tokens = out.shape[1]
    heads = values.shape[0] // tokens
    wide[...] = values[...].astype(jnp.float32)
    left = jnp.concatenate(
        [wide[pl.ds(h, tokens, stride=heads), :] for h in range(heads)], axis=-1
    ).astype(jnp.bfloat16)
    terms = jnp.dot(left, weight[...], preferred_element_type=jnp.float32)
    width = out.shape[2]
    for i in range(out.shape[0]):
        out[i] = terms[:, i * width : (i + 1) * width]


def whole(count):
    return [pl.BlockSpec(memory_space=pltpu.VMEM)] * count


def in_hbm(array):
    return pltpu.with_memory_space_constraint(array, pltpu.HBM)


def kernel_params(mebibytes):
    return pltpu.CompilerParams(vmem_limit_bytes=mebibytes << 20)


def shards(query_nope, query_rope, latent_cache, lengths, key_weight, value_weight, output_weight):
    n_seq, n_grp = lax.axis_size("seq"), lax.axis_size("grp")
    requests, drafts, heads, nope = query_nope.shape
    rope = query_rope.shape[3]
    latent = key_weight.shape[2]
    positions, width = latent_cache.shape[1:]
    factor = float(nope + rope) ** (-0.5)
    rows = drafts * heads
    assert requests == n_grp

    def partner(k):
        if n_grp & (n_grp - 1) == 0:
            return lambda i: i ^ k
        return lambda i: (k - i) % n_grp

    partners = [partner(k) for k in range(n_grp)]
    by_width = jnp.swapaxes(latent_cache, 1, 2)
    smem = pl.BlockSpec(memory_space=pltpu.SMEM)
    hbm = pl.BlockSpec(memory_space=pltpu.HBM)
    routes = [[(i, other(i)) for i in range(n_grp)] for other in partners]
    kept = [k for k in range(n_grp) if all(i == j for i, j in routes[k])]
    pieces = pl.pallas_call(
        functools.partial(pick_kernel, partners),
        out_shape=[jax.ShapeDtypeStruct((width, positions), jnp.bfloat16)] * n_grp,
        in_specs=[hbm],
        out_specs=whole(n_grp),
        scratch_shapes=[pltpu.SemaphoreType.DMA((n_grp,))],
        compiler_params=kernel_params(4),
        name="pick",
    )(in_hbm(by_width))
    caches = []
    for k, piece in enumerate(pieces):
        caches.append(piece if k in kept else lax.ppermute(piece, "grp", routes[k]))
    queries = pl.pallas_call(
        absorb_kernel,
        out_shape=jax.ShapeDtypeStruct((n_seq, rows, width), jnp.bfloat16),
        in_specs=[hbm] * 3,
        out_specs=whole(1)[0],
        scratch_shapes=[
            pltpu.VMEM((rows, nope), jnp.bfloat16),
            pltpu.VMEM((rows, rope), jnp.bfloat16),
            pltpu.VMEM(key_weight.shape, jnp.bfloat16),
            pltpu.SemaphoreType.DMA((3,)),
        ],
        compiler_params=kernel_params(8),
        name="absorb",
    )(
        in_hbm(query_nope.reshape(requests, rows, nope)),
        in_hbm(query_rope.reshape(requests, rows, rope)),
        in_hbm(key_weight),
    )
    queries = lax.all_to_all(queries, "seq", 0, 0, tiled=True)

    partial = pl.pallas_call(
        functools.partial(attention_kernel, factor, latent, heads, drafts, partners),
        out_shape=jax.ShapeDtypeStruct((n_seq * rows, latent + LANES), jnp.bfloat16),
        in_specs=[smem] + whole(1 + n_grp),
        out_specs=whole(1)[0],
        compiler_params=kernel_params(12),
        cost_estimate=pl.CostEstimate(flops=6 * 10**9, transcendentals=0, bytes_accessed=3 << 20),
        name="attention",
    )(lengths, queries.reshape(n_seq * rows, width), *caches)

    received = lax.all_to_all(partial.reshape(n_seq, rows, latent + LANES), "seq", 0, 0, tiled=True)
    values = pl.pallas_call(
        functools.partial(merge_kernel, latent),
        out_shape=jax.ShapeDtypeStruct((rows, value_weight.shape[2]), jnp.bfloat16),
        in_specs=whole(2),
        out_specs=whole(1)[0],
        compiler_params=kernel_params(8),
        name="merge",
    )(received, value_weight)
    values = lax.all_gather(values, "grp", axis=0, tiled=True)

    tokens = requests * drafts
    columns = output_weight.shape[1] // n_seq
    terms = pl.pallas_call(
        project_kernel,
        out_shape=jax.ShapeDtypeStruct((n_seq, tokens, columns), jnp.float32),
        in_specs=whole(2),
        out_specs=whole(1)[0],
        scratch_shapes=[pltpu.VMEM(values.shape, jnp.float32)],
        compiler_params=kernel_params(12),
        name="project",
    )(values, output_weight)
    terms = lax.all_to_all(terms, "seq", 0, 0, tiled=True)
    mixed = jnp.sum(terms, axis=0).astype(jnp.bfloat16)
    return mixed.reshape(requests, drafts, columns)


def solution(mesh):
    in_specs = (
        P(None, None, "seq", None),
        P(None, None, "seq", None),
        P(None, ("seq", "grp"), None),
        P(),
        P("seq", None, None),
        P("seq", None, None),
        P("seq", "grp"),
    )
    out_specs = P(None, None, ("grp", "seq"))
    return jax.shard_map(shards, mesh=mesh, in_specs=in_specs, out_specs=out_specs, check_vma=False)
```

time: 68.3 us -> 63.5 us (0.930)
  local copies, waits for them, and re-layouts: 5.94 us -> 0.62 us
  Pallas kernels: 2.49 us -> 7.48 us
  matrix products: 4.89 us -> 0 us
  waiting for transfers between devices: 12.5 us -> 13.3 us
    dot_general x3 -> x0, matrix products: 4.89 us -> none  [the longest x1 4.14 us: shards(): terms = jnp.dot(values, output_weight, preferred_element_type=jnp.float32)]
    pallas_call x1 -> x4, Pallas kernels: 2.19 us -> 6.82 us  [the longest x1 2.82 us: shards(): pl.pallas_call(absorb_kernel, out_shape=jax.ShapeDtypeStruct((n_seq, rows...]
    squeeze x1 -> x0, local copies, waits for them, and re-layouts: 2.2 us -> none  [request(): return lax.dynamic_index_in_dim(array, index, 0, False)]
    dynamic_slice x3 -> x0, local copies, waits for them, and re-layouts: 2.14 us -> none  [request(): return lax.dynamic_index_in_dim(array, index, 0, False)]
    ppermute x3, waiting for transfers between devices: 12.5 us -> 13.3 us  [shards(): caches.append(piece if k in kept else lax.ppermute(piece, 'grp', routes[k]))]
    broadcast_in_dim x1 -> x0, local copies, waits for them, and re-layouts: 0.76 us -> none  [shards(): jnp.broadcast_to(own, (n_seq,) + own.shape[1:])]
  transfers between devices with their start and end apart: 4 -> 4, of which waited for: 2 -> 2; matrix products, arithmetic and copies ran while one was open for 4% -> 0% of each run, Pallas kernels for 0% -> 2%
where the time goes in v2:
time: 63.5 us; the launch traced here: 63.2 us
  blocking collectives  32.4 us (51%)
  waiting for transfers between devices  13.3 us (21%)
  starting transfers between devices  9.24 us (15%)
  Pallas kernels  7.48 us (12%)
    all_to_all x1, blocking collectives, shards(): lax.all_to_all(partial.reshape(n_seq, rows, latent + LANES), 'seq', 0, 0,...  17.5 us
    ppermute x3, waiting for transfers between devices, shards(): caches.append(piece if k in kept else lax.ppermute(piece, 'grp', routes[k]))  13.3 us
    all_to_all x1, blocking collectives, shards(): terms = lax.all_to_all(terms, 'seq', 0, 0, tiled=True)  9.7 us
    all_to_all x1, starting transfers between devices, shards(): queries = lax.all_to_all(queries, 'seq', 0, 0, tiled=True)  7.32 us
    all_gather x1, blocking collectives, shards(): values = lax.all_gather(values, 'grp', axis=0, tiled=True)  5.19 us
    pallas_call x1, Pallas kernels, shards(): pl.pallas_call(absorb_kernel, out_shape=jax.ShapeDtypeStruct((n_seq, rows...  2.82 us
    ppermute x3, starting transfers between devices, shards(): caches.append(piece if k in kept else lax.ppermute(piece, 'grp', routes[k]))  1.92 us
    pallas_call x1, Pallas kernels, shards(): pl.pallas_call(functools.partial(attention_kernel, factor, latent, heads,...  1.6 us
  transfers between devices with their start and end apart: 4, of which 2 were waited for; matrix products, arithmetic and copies ran while one was open for 0% of the time, Pallas kernels for 2%

profile of v2, /device:TPU:0, one launch (start us, length us, event | category | flops | bytes accessed | tf_op | source)
XLA Modules:
  0.0 63.2 jit_solution(1290832892297258080)
XLA Ops:
  0.0 0.0 copy-start.1
  0.0 2.8 %absorb.1 = bf16[8,32,576]{2,1,0:T(8,128)(2,1)} custom-call(bf16[4,32,128]{2,1,0:T(8,128)(2,1)} %bitcast.10, bf16[4,32,64]{2,1,0:T(8,128)(2,1)} %bitcast.11, bf16[16,128,512]{2,1,0:T(8,128)(2,1)} %weight.3), custom_call_target="tpu_custom_call" | custom-call | tf_op jit(solution)/shard_map/absorb/pallas_call | solution.py:172
  2.8 7.3 %all-to-all-start = ((bf16[8,32,576]{2,1,0:T(8,128)(2,1)}), bf16[8,32,576]{2,1,0:T(8,128)(2,1)S(1)}, u32[]{:S(2)}, u32[]{:S(2)}) async-start(bf16[8,32,576]{2,1,0:T(8,128)(2,1)} %absorb.1), calls=%async_computation | async-start | bytes 655360 | tf_op jit(solution)/shard_map/all_to_all | solution.py:190
  10.2 1.3 %pick.1 = (bf16[576,256]{1,0:T(8,128)(2,1)S(1)}, bf16[576,256]{1,0:T(8,128)(2,1)S(1)}, bf16[576,256]{1,0:T(8,128)(2,1)S(1)}, bf16[576,256]{1,0:T(8,128)(2,1)S(1)}) custom-call(bf16[4,576,256]{2,1,0:T(8,128)(2,1)} %bitcast.9), custom_call_target="tpu_custom_call" | custom-call | tf_op jit(solution)/shard_map/pick/pallas_call | solution.py:160
  11.4 0.1 collective-permute-start
  11.5 1.6 %collective-permute-start.1 = (bf16[576,256]{1,0:T(8,128)(2,1)S(1)}, bf16[576,256]{1,0:T(8,128)(2,1)S(1)}, u32[]{:S(2)}, u32[]{:S(2)}) collective-permute-start(bf16[576,256]{1,0:T(8,128)(2,1)S(1)} %get-tuple-element.11), channel_id=1, source_target_pairs={{0,2},{1,3},{2,0},{3,1},{4,6},{5,7},{6,4},{7,5},{8,10},{9,11},{10,... | collective-permute-start | bytes 884744 | tf_op jit(solution)/shard_map/ppermute | solution.py:171
  13.1 0.3 collective-permute-start.2
  13.4 0.0 collective-permute-done.refs_1_
  13.4 8.1 %collective-permute-done.1.refs_2_ = bf16[576,256]{1,0:T(8,128)(2,1)S(1)} collective-permute-done((bf16[576,256]{1,0:T(8,128)(2,1)S(1)}, bf16[576,256]{1,0:T(8,128)(2,1)S(1)}, u32[]{:S(2)}, u32[]{:S(2)}) %collective-permute-start.1) | collective-permute-done | bytes 294944 | tf_op jit(solution)/shard_map/ppermute | solution.py:171
  21.5 5.2 %collective-permute-done.2.refs_3_ = bf16[576,256]{1,0:T(8,128)(2,1)S(1)} collective-permute-done((bf16[576,256]{1,0:T(8,128)(2,1)S(1)}, bf16[576,256]{1,0:T(8,128)(2,1)S(1)}, u32[]{:S(2)}, u32[]{:S(2)}) %collective-permute-start.2) | collective-permute-done | bytes 294944 | tf_op jit(solution)/shard_map/ppermute | solution.py:171
  26.7 0.0 all-to-all-done
  26.7 0.0 slice-start
  26.7 0.0 copy-done.1
  26.7 0.0 copy-start
  26.7 0.0 slice-start.1
  26.7 1.6 %attention.1 = bf16[256,640]{1,0:T(8,128)(2,1)S(1)} custom-call(s32[4]{0:T(128)S(1)} %copy-done.1, bf16[256,576]{1,0:T(8,128)(2,1)S(1)} %bitcast.7, bf16[576,256]{1,0:T(8,128)(2,1)S(1)} %get-tuple-element.9.refs_0_, bf16[576,256]{1,0:T(8,128)(2,1)S(1)} %collective-permute-done.refs_1_, bf16[576,256]{1,0:T(8,128)(2,1)S(1)} %collective-permute-done.1.refs_2_, ...), custom_call_target="tpu_custom_call" | custom-call | flops 6000000000 | bytes 3145728 | tf_op jit(solution)/shard_map/attention/pallas_call | solution.py:192
  28.3 17.5 %all_to_all.15.received = bf16[8,32,640]{2,1,0:T(8,128)(2,1)S(1)} all-to-all(bf16[8,32,640]{2,1,0:T(8,128)(2,1)S(1)} %bitcast.8), channel_id=1, replica_groups=mesh['seq'=8,'grp'=4] {'seq'}, dimensions={0} | all-to-all | bytes 655360 | tf_op jit(solution)/shard_map/all_to_all | solution.py:202
  45.8 0.0 copy-done
  45.8 0.7 %merge.1 = bf16[32,128]{1,0:T(8,128)(2,1)S(1)} custom-call(bf16[8,32,640]{2,1,0:T(8,128)(2,1)S(1)} %all_to_all.15.received, bf16[16,512,128]{2,1,0:T(8,128)(2,1)S(1)} %copy-done), custom_call_target="tpu_custom_call" | custom-call | tf_op jit(solution)/shard_map/merge/pallas_call | solution.py:203
  46.5 5.2 %all_gather.3.values = bf16[128,128]{1,0:T(8,128)(2,1)S(1)} all-gather(bf16[32,128]{1,0:T(8,128)(2,1)S(1)} %merge.1), channel_id=1, replica_groups=mesh['seq'=8,'grp'=4] {'grp'}, dimensions={0}, use_global_device_ids=true | all-gather | bytes 40960 | tf_op jit(solution)/shard_map/all_gather | solution.py:211
  51.7 0.0 slice-done
  51.7 0.0 slice-done.1
  51.7 1.1 %project.1 = f32[8,8,224]{2,1,0:T(8,128)S(1)} custom-call(bf16[128,128]{1,0:T(8,128)(2,1)S(1)} %all_gather.3.values, bf16[2048,1792]{1,0:T(8,128)(2,1)S(1)} %bitcast.6), custom_call_target="tpu_custom_call" | custom-call | tf_op jit(solution)/shard_map/project/pallas_call | solution.py:215
  52.8 9.7 %all_to_all.16 = f32[8,8,224]{2,1,0:T(8,128)S(1)} all-to-all(f32[8,8,224]{2,1,0:T(8,128)S(1)} %project.1), channel_id=1, replica_groups=mesh['seq'=8,'grp'=4] {'seq'}, dimensions={0} | all-to-all | bytes 114688 | tf_op jit(solution)/shard_map/all_to_all | solution.py:224
  62.5 0.6 convert_element_type.8
  (2 shorter events, 0.0 us)
Async XLA Ops:
  0.0 26.7 %copy-start.1 = (s32[4]{0:T(128)S(1)}, s32[4]{0:T(128)}, u32[]{:S(2)}) copy-start(s32[4]{0:T(128)} %lengths.1) | copy-start | bytes 52
  2.8 23.9 %all-to-all-start = ((bf16[8,32,576]{2,1,0:T(8,128)(2,1)}), bf16[8,32,576]{2,1,0:T(8,128)(2,1)S(1)}, u32[]{:S(2)}, u32[]{:S(2)}) async-start(bf16[8,32,576]{2,1,0:T(8,128)(2,1)} %absorb.1), calls=%async_computation | async-start | bytes 655360 | tf_op jit(solution)/shard_map/all_to_all | solution.py:190
  11.4 1.9 %collective-permute-start = (bf16[576,256]{1,0:T(8,128)(2,1)S(1)}, bf16[576,256]{1,0:T(8,128)(2,1)S(1)}, u32[]{:S(2)}, u32[]{:S(2)}) collective-permute-start(bf16[576,256]{1,0:T(8,128)(2,1)S(1)} %get-tuple-element.10), channel_id=1, source_target_pairs={{0,1},{1,0},{2,3},{3,2},{4,5},{5,4},{6,7},{7,6},{8,9},{9,8},{10,11... | collective-permute-start | bytes 884744 | tf_op jit(solution)/shard_map/ppermute | solution.py:171
  11.5 9.9 %collective-permute-start.1 = (bf16[576,256]{1,0:T(8,128)(2,1)S(1)}, bf16[576,256]{1,0:T(8,128)(2,1)S(1)}, u32[]{:S(2)}, u32[]{:S(2)}) collective-permute-start(bf16[576,256]{1,0:T(8,128)(2,1)S(1)} %get-tuple-element.11), channel_id=1, source_target_pairs={{0,2},{1,3},{2,0},{3,1},{4,6},{5,7},{6,4},{7,5},{8,10},{9,11},{10,... | collective-permute-start | bytes 884744 | tf_op jit(solution)/shard_map/ppermute | solution.py:171
  13.1 13.6 %collective-permute-start.2 = (bf16[576,256]{1,0:T(8,128)(2,1)S(1)}, bf16[576,256]{1,0:T(8,128)(2,1)S(1)}, u32[]{:S(2)}, u32[]{:S(2)}) collective-permute-start(bf16[576,256]{1,0:T(8,128)(2,1)S(1)} %get-tuple-element.12), channel_id=1, source_target_pairs={{0,3},{1,2},{2,1},{3,0},{4,7},{5,6},{6,5},{7,4},{8,11},{9,10},{10,... | collective-permute-start | bytes 884744 | tf_op jit(solution)/shard_map/ppermute | solution.py:171
  26.7 25.0 %slice-start = ((s8[7340032]{0:T(1024)(128)(4,1)}), s8[4194304]{0:T(1024)(128)(4,1)S(1)}, s32[]{:S(2)}) async-start(s8[7340032]{0:T(1024)(128)(4,1)} %bitcast.5), calls=%async_computation.3 | async-start | bytes 8388608
  26.7 19.1 %copy-start = (bf16[16,512,128]{2,1,0:T(8,128)(2,1)S(1)}, bf16[16,512,128]{2,1,0:T(8,128)(2,1)}, u32[]{:S(2)}) copy-start(bf16[16,512,128]{2,1,0:T(8,128)(2,1)} %weight.4) | copy-start | bytes 6291460
  26.7 25.0 %slice-start.1 = ((s8[7340032]{0:T(1024)(128)(4,1)}), s8[3145728]{0:T(1024)(128)(4,1)S(1)}, s32[]{:S(2)}) async-start(s8[7340032]{0:T(1024)(128)(4,1)} %bitcast.5), calls=%async_computation.4 | async-start | bytes 6291456

commit v3 on v2

--- a/solution.py
+++ b/solution.py
@@ -10,6 +10,7 @@
 
 NEGATIVE = -1e30
 LANES = 128
+STATS = 8
 
 
 def split3(x):
@@ -19,17 +20,48 @@
     return high, middle, rest - middle
 
 
-def attention_kernel(factor, latent, heads, drafts, partners, lengths, query, *refs):
+def chunks(width):
+    return range(width // LANES)
+
+
+def packs(n_seq, drafts, heads, latent, rope):
+    rows = drafts * heads
+    return (
+        heads % 16 == 0
+        and latent % LANES == 0
+        and drafts * rope == LANES
+        and LANES % rows == 0
+        and n_seq * rows % LANES == 0
+    )
+
+
+def unpack_queries(query, latent, heads, drafts):
+    n_seq, _, lanes = query.shape
+    rows = drafts * heads
+    parts = [query[:, c * rows : (c + 1) * rows, :] for c in chunks(latent)]
+    tail = query[:, len(parts) * rows :, :]
+    owner = lax.broadcasted_iota(jnp.int32, tail.shape, 2) // (lanes // drafts)
+    zero = jnp.zeros_like(tail)
+    parts.append(
+        jnp.concatenate([jnp.where(owner == t, tail, zero) for t in range(drafts)], axis=1)
+    )
+    return jnp.concatenate([part.reshape(n_seq * rows, lanes) for part in parts], axis=-1)
+
+
+def attention_kernel(factor, latent, heads, drafts, partners, packed, lengths, query, *refs):
     caches, out = refs[:-1], refs[-1]
-    rows = query.shape[0]
+    rows = query.shape[0] * drafts * heads if packed else query.shape[0]
     width = caches[0].shape[1]
     seq, grp = lax.axis_index("seq"), lax.axis_index("grp")
     token = (lax.broadcasted_iota(jnp.int32, (rows, 1), 0) // heads) % drafts
     limit = lengths[grp] - drafts + 1 + token
-    queries = query[...]
+    queries = unpack_queries(query, latent, heads, drafts) if packed else query[...]
     scores = []
     for j, cache in enumerate(caches):
-        raw = jnp.dot(queries, cache[...], preferred_element_type=jnp.float32) * factor
+        keys = cache[...]
+        if packed:
+            keys = jnp.concatenate([keys] + [cache[latent:, :]] * (drafts - 1), axis=0)
+        raw = jnp.dot(queries, keys, preferred_element_type=jnp.float32) * factor
         offset = (seq * len(caches) + partners[j](grp)) * width
         places = offset + lax.broadcasted_iota(jnp.int32, (rows, width), 1)
         scores.append(jnp.where(places < limit, raw, NEGATIVE))
@@ -45,12 +77,23 @@
             (((1,), (1,)), ((), ())),
             preferred_element_type=jnp.float32,
         )
-    out[:, :latent] = (summed / total).astype(jnp.bfloat16)
+    result = (summed / total).astype(jnp.bfloat16)
     lane = lax.broadcasted_iota(jnp.int32, (rows, LANES), 1)
-    packed = jnp.zeros((rows, LANES), jnp.float32)
+    stats = jnp.zeros((rows, LANES), jnp.float32)
     for i, piece in enumerate(split3(top) + split3(total)):
-        packed = jnp.where(lane == i, piece, packed)
-    out[:, latent:] = packed.astype(jnp.bfloat16)
+        stats = jnp.where(lane == i, piece, stats)
+    if not packed:
+        out[:, :latent] = result
+        out[:, latent:] = stats.astype(jnp.bfloat16)
+        return
+    block = drafts * heads
+    by_stat = stats.T[:STATS].astype(jnp.bfloat16)
+    for i in range(rows // block):
+        for c in chunks(latent):
+            lanes = slice(c * LANES, (c + 1) * LANES)
+            out[i, c * block : (c + 1) * block, :] = result[i * block : (i + 1) * block, lanes]
+        start = i * block // LANES * LANES
+        out[i, len(chunks(latent)) * block :, :] = by_stat[:, start : start + LANES]
 
 
 def stacked(array, heads):
@@ -73,41 +116,72 @@
         copy.wait()
 
 
-def absorb_kernel(nope, rope, weight, queries, nope_block, rope_block, weights, sems):
+def absorb_kernel(drafts, packed, nope, rope, weight, queries):
     grp = lax.axis_index("grp")
-    copies = [
-        pltpu.make_async_copy(weight, weights, sems.at[0]),
-        pltpu.make_async_copy(nope.at[grp], nope_block, sems.at[1]),
-        pltpu.make_async_copy(rope.at[grp], rope_block, sems.at[2]),
-    ]
-    for copy in copies:
-        copy.start()
-    for copy in copies[::-1]:
-        copy.wait()
-    heads, depth, latent = weights.shape
+    heads, depth, latent = weight.shape
     absorbed = jnp.dot(
-        stacked(nope_block[...], heads),
-        weights[...].reshape(heads * depth, latent),
+        stacked(nope[grp], heads),
+        weight[...].reshape(heads * depth, latent),
         preferred_element_type=jnp.float32,
     ).astype(jnp.bfloat16)
-    tail = rope_block[...]
+    tail = rope[grp]
+    if not packed:
+        for i in range(queries.shape[0]):
+            queries[i, :, :latent] = absorbed
+            queries[i, :, latent:] = tail
+        return
+    parts = [absorbed[:, c * LANES : (c + 1) * LANES] for c in chunks(latent)]
+    parts.append(
+        jnp.concatenate([tail[t * heads : (t + 1) * heads] for t in range(drafts)], axis=-1)
+    )
+    block = jnp.concatenate(parts, axis=0)
     for i in range(queries.shape[0]):
-        queries[i, :, :latent] = absorbed
-        queries[i, :, latent:] = tail
-
-
-def merge_kernel(latent, received, weight, out):
-    block = received[...].astype(jnp.float32)
-    stats = block[:, :, latent:]
-    top = (stats[:, :, 0:1] + stats[:, :, 1:2]) + stats[:, :, 2:3]
-    total = (stats[:, :, 3:4] + stats[:, :, 4:5]) + stats[:, :, 5:6]
-    peak = jnp.max(top, axis=0, keepdims=True)
-    share = total * jnp.exp(top - peak)
-    numerator = jnp.sum(share * block[:, :, :latent], axis=0)
-    merged = (numerator / jnp.sum(share, axis=0)).astype(jnp.bfloat16)
+        queries[i] = block
+
+
+def merge_kernel(latent, packed, received, weight, out, *scratch):
     heads, depth, width = weight.shape
-    weights = weight[...].reshape(heads * depth, width)
-    values = jnp.dot(stacked(merged, heads), weights, preferred_element_type=jnp.float32)
+    rows = out.shape[0]
+    sources = received.shape[0]
+    if packed:
+        turned = scratch[0]
+        first = len(chunks(latent)) * rows
+        stats = received[:, first:, :].astype(jnp.float32).reshape(sources * STATS, LANES)
+        turned[...] = stats.T
+        start = lax.axis_index("seq") * rows % LANES
+        own = turned[pl.ds(pl.multiple_of(start, rows), rows), :]
+        columns = [[own[:, j * STATS + i : j * STATS + i + 1] for i in range(6)] for j in range(sources)]
+        parts = [
+            [received[j, c * rows : (c + 1) * rows, :] for j in range(sources)]
+            for c in chunks(latent)
+        ]
+    else:
+        block = received[...]
+        stats = block[:, :, latent:].astype(jnp.float32)
+        columns = [[stats[j, :, i : i + 1] for i in range(6)] for j in range(sources)]
+        parts = [[block[j, :, :latent] for j in range(sources)]]
+    tops = [(column[0] + column[1]) + column[2] for column in columns]
+    peak = functools.reduce(jnp.maximum, tops)
+    shares = [
+        ((column[3] + column[4]) + column[5]) * jnp.exp(top - peak)
+        for column, top in zip(columns, tops)
+    ]
+    summed = functools.reduce(jnp.add, shares)
+    merged = jnp.concatenate(
+        [
+            functools.reduce(
+                jnp.add, [share * piece.astype(jnp.float32) for share, piece in zip(shares, part)]
+            )
+            / summed
+            for part in parts
+        ],
+        axis=-1,
+    ).astype(jnp.bfloat16)
+    values = jnp.dot(
+        stacked(merged, heads),
+        weight[...].reshape(heads * depth, width),
+        preferred_element_type=jnp.float32,
+    )
     out[...] = values.astype(jnp.bfloat16)
 
 
@@ -121,7 +195,7 @@
     terms = jnp.dot(left, weight[...], preferred_element_type=jnp.float32)
     width = out.shape[2]
     for i in range(out.shape[0]):
-        out[i] = terms[:, i * width : (i + 1) * width]
+        out[i] = terms[:, i * width : (i + 1) * width].astype(out.dtype)
 
 
 def whole(count):
@@ -145,6 +219,9 @@
     factor = float(nope + rope) ** (-0.5)
     rows = drafts * heads
     assert requests == n_grp
+    packed = packs(n_seq, drafts, heads, latent, rope)
+    asked = (rows * len(chunks(latent)) + heads, LANES) if packed else (rows, width)
+    given = (rows * len(chunks(latent)) + STATS, LANES) if packed else (rows, latent + LANES)
 
     def partner(k):
         if n_grp & (n_grp - 1) == 0:
@@ -164,47 +241,45 @@
         out_specs=whole(n_grp),
         scratch_shapes=[pltpu.SemaphoreType.DMA((n_grp,))],
         compiler_params=kernel_params(4),
+        cost_estimate=pl.CostEstimate(flops=3 * 10**9, transcendentals=0, bytes_accessed=2 << 20),
         name="pick",
     )(in_hbm(by_width))
     caches = []
     for k, piece in enumerate(pieces):
         caches.append(piece if k in kept else lax.ppermute(piece, "grp", routes[k]))
     queries = pl.pallas_call(
-        absorb_kernel,
-        out_shape=jax.ShapeDtypeStruct((n_seq, rows, width), jnp.bfloat16),
-        in_specs=[hbm] * 3,
+        functools.partial(absorb_kernel, drafts, packed),
+        out_shape=jax.ShapeDtypeStruct((n_seq,) + asked, jnp.bfloat16),
+        in_specs=whole(3),
         out_specs=whole(1)[0],
-        scratch_shapes=[
-            pltpu.VMEM((rows, nope), jnp.bfloat16),
-            pltpu.VMEM((rows, rope), jnp.bfloat16),
-            pltpu.VMEM(key_weight.shape, jnp.bfloat16),
-            pltpu.SemaphoreType.DMA((3,)),
-        ],
         compiler_params=kernel_params(8),
         name="absorb",
     )(
-        in_hbm(query_nope.reshape(requests, rows, nope)),
-        in_hbm(query_rope.reshape(requests, rows, rope)),
-        in_hbm(key_weight),
+        query_nope.reshape(requests, rows, nope),
+        query_rope.reshape(requests, rows, rope),
+        key_weight,
     )
     queries = lax.all_to_all(queries, "seq", 0, 0, tiled=True)
 
     partial = pl.pallas_call(
-        functools.partial(attention_kernel, factor, latent, heads, drafts, partners),
-        out_shape=jax.ShapeDtypeStruct((n_seq * rows, latent + LANES), jnp.bfloat16),
+        functools.partial(attention_kernel, factor, latent, heads, drafts, partners, packed),
+        out_shape=jax.ShapeDtypeStruct(
+            (n_seq,) + given if packed else (n_seq * rows,) + given[1:], jnp.bfloat16
+        ),
         in_specs=[smem] + whole(1 + n_grp),
         out_specs=whole(1)[0],
         compiler_params=kernel_params(12),
         cost_estimate=pl.CostEstimate(flops=6 * 10**9, transcendentals=0, bytes_accessed=3 << 20),
         name="attention",
-    )(lengths, queries.reshape(n_seq * rows, width), *caches)
-
-    received = lax.all_to_all(partial.reshape(n_seq, rows, latent + LANES), "seq", 0, 0, tiled=True)
+    )(lengths, queries if packed else queries.reshape(n_seq * rows, width), *caches)
+
+    received = lax.all_to_all(partial.reshape((n_seq,) + given), "seq", 0, 0, tiled=True)
     values = pl.pallas_call(
-        functools.partial(merge_kernel, latent),
+        functools.partial(merge_kernel, latent, packed),
         out_shape=jax.ShapeDtypeStruct((rows, value_weight.shape[2]), jnp.bfloat16),
         in_specs=whole(2),
         out_specs=whole(1)[0],
+        scratch_shapes=[pltpu.VMEM((LANES, n_seq * STATS), jnp.float32)] * packed,
         compiler_params=kernel_params(8),
         name="merge",
     )(received, value_weight)
@@ -214,7 +289,7 @@
     columns = output_weight.shape[1] // n_seq
     terms = pl.pallas_call(
         project_kernel,
-        out_shape=jax.ShapeDtypeStruct((n_seq, tokens, columns), jnp.float32),
+        out_shape=jax.ShapeDtypeStruct((n_seq, tokens, columns), jnp.bfloat16),
         in_specs=whole(2),
         out_specs=whole(1)[0],
         scratch_shapes=[pltpu.VMEM(values.shape, jnp.float32)],
@@ -222,7 +297,7 @@
         name="project",
     )(values, output_weight)
     terms = lax.all_to_all(terms, "seq", 0, 0, tiled=True)
-    mixed = jnp.sum(terms, axis=0).astype(jnp.bfloat16)
+    mixed = jnp.sum(terms.astype(jnp.float32), axis=0).astype(jnp.bfloat16)
     return mixed.reshape(requests, drafts, columns)
 
 

time: 63.5 us -> 64.1 us (level)
  local copies, waits for them, and re-layouts: 0.62 us -> 3.73 us
  blocking collectives: 32.4 us -> 31.1 us
  Pallas kernels: 7.48 us -> 6.19 us
    unnamed x8 -> x14, local copies, waits for them, and re-layouts: 0.02 us -> 3.12 us
    pallas_call x2, Pallas kernels: 3.49 us -> 2.18 us  [the longest x1 1.2 us: shards(): pl.pallas_call(functools.partial(absorb_kernel, drafts, packed), out_shap...]
    all_to_all x1, blocking collectives: 17.5 us -> 16.6 us  [shards(): lax.all_to_all(partial.reshape((n_seq,) + given), 'seq', 0, 0, tiled=True)]
where the time goes in v3:
time: 64.1 us; the launch traced here: 63.7 us
  blocking collectives  31.1 us (49%)
  waiting for transfers between devices  13.3 us (21%)
  starting transfers between devices  9.23 us (14%)
  Pallas kernels  6.19 us (10%)
  local copies, waits for them, and re-layouts  3.73 us (6%)
    all_to_all x1, blocking collectives, shards(): lax.all_to_all(partial.reshape((n_seq,) + given), 'seq', 0, 0, tiled=True)  16.6 us
    ppermute x3, waiting for transfers between devices, shards(): caches.append(piece if k in kept else lax.ppermute(piece, 'grp', routes[k]))  13.3 us
    all_to_all x1, blocking collectives, shards(): terms = lax.all_to_all(terms, 'seq', 0, 0, tiled=True)  9.28 us
    all_to_all x1, starting transfers between devices, shards(): queries = lax.all_to_all(queries, 'seq', 0, 0, tiled=True)  7.31 us
    all_gather x1, blocking collectives, shards(): values = lax.all_gather(values, 'grp', axis=0, tiled=True)  5.19 us
    unnamed x14, local copies, waits for them, and re-layouts  3.12 us
    ppermute x3, starting transfers between devices, shards(): caches.append(piece if k in kept else lax.ppermute(piece, 'grp', routes[k]))  1.92 us
    pallas_call x1, Pallas kernels, shards(): pl.pallas_call(functools.partial(attention_kernel, factor, latent, heads,...  1.6 us
  transfers between devices with their start and end apart: 4, of which 2 were waited for; matrix products, arithmetic and copies ran while one was open for 0% of the time, Pallas kernels for 2%

profile of v3, /device:TPU:0, one launch (start us, length us, event | category | flops | bytes accessed | tf_op | source)
XLA Modules:
  0.0 63.7 jit_solution(14639941632929843223)
XLA Ops:
  0.0 0.0 copy-start
  0.0 1.6 %copy-done = bf16[16,128,512]{2,1,0:T(8,128)(2,1)S(1)} copy-done((bf16[16,128,512]{2,1,0:T(8,128)(2,1)S(1)}, bf16[16,128,512]{2,1,0:T(8,128)(2,1)}, u32[]{:S(2)}) %copy-start) | copy-done | bytes 2097176
  1.6 0.0 copy-start.2
  1.6 0.8 %copy-done.2 = bf16[4,2,16,128]{3,2,1,0:T(8,128)(2,1)S(1)} copy-done((bf16[4,2,16,128]{3,2,1,0:T(8,128)(2,1)S(1)}, bf16[4,2,16,128]{3,2,1,0:T(8,128)(2,1)}, u32[]{:S(2)}) %copy-start.2) | copy-done | bytes 32792
  2.4 0.0 copy-start.3
  2.4 0.8 %copy-done.3 = bf16[4,2,16,64]{3,2,1,0:T(8,128)(2,1)S(1)} copy-done((bf16[4,2,16,64]{3,2,1,0:T(8,128)(2,1)S(1)}, bf16[4,2,16,64]{3,2,1,0:T(8,128)(2,1)}, u32[]{:S(2)}) %copy-start.3) | copy-done | bytes 16408
  3.1 1.2 %absorb.1 = bf16[8,144,128]{2,1,0:T(8,128)(2,1)} custom-call(bf16[4,32,128]{2,1,0:T(8,128)(2,1)S(1)} %bitcast.5, bf16[4,32,64]{2,1,0:T(8,128)(2,1)S(1)} %bitcast.6, bf16[16,128,512]{2,1,0:T(8,128)(2,1)S(1)} %copy-done), custom_call_target="tpu_custom_call" | custom-call | tf_op jit(solution)/shard_map/absorb/pallas_call | solution.py:250
  4.3 7.3 %all-to-all-start = ((bf16[8,144,128]{2,1,0:T(8,128)(2,1)}), bf16[8,144,128]{2,1,0:T(8,128)(2,1)S(1)}, u32[]{:S(2)}, u32[]{:S(2)}) async-start(bf16[8,144,128]{2,1,0:T(8,128)(2,1)} %absorb.1), calls=%async_computation | async-start | bytes 589824 | tf_op jit(solution)/shard_map/all_to_all | solution.py:262
  11.6 0.0 copy-start.4
  11.6 1.3 %pick.1 = (bf16[576,256]{1,0:T(8,128)(2,1)S(1)}, bf16[576,256]{1,0:T(8,128)(2,1)S(1)}, bf16[576,256]{1,0:T(8,128)(2,1)S(1)}, bf16[576,256]{1,0:T(8,128)(2,1)S(1)}) custom-call(bf16[4,576,256]{2,1,0:T(8,128)(2,1)} %bitcast.7), custom_call_target="tpu_custom_call" | custom-call | flops 3000000000 | bytes 2097152 | tf_op jit(solution)/shard_map/pick/pallas_call | solution.py:237
  12.9 0.1 collective-permute-start
  13.0 1.6 %collective-permute-start.1 = (bf16[576,256]{1,0:T(8,128)(2,1)S(1)}, bf16[576,256]{1,0:T(8,128)(2,1)S(1)}, u32[]{:S(2)}, u32[]{:S(2)}) collective-permute-start(bf16[576,256]{1,0:T(8,128)(2,1)S(1)} %get-tuple-element.11), channel_id=1, source_target_pairs={{0,2},{1,3},{2,0},{3,1},{4,6},{5,7},{6,4},{7,5},{8,10},{9,11},{10,... | collective-permute-start | bytes 884744 | tf_op jit(solution)/shard_map/ppermute | solution.py:249
  14.5 0.3 collective-permute-start.2
  14.8 0.0 collective-permute-done.refs_1_
  14.8 8.1 %collective-permute-done.1.refs_2_ = bf16[576,256]{1,0:T(8,128)(2,1)S(1)} collective-permute-done((bf16[576,256]{1,0:T(8,128)(2,1)S(1)}, bf16[576,256]{1,0:T(8,128)(2,1)S(1)}, u32[]{:S(2)}, u32[]{:S(2)}) %collective-permute-start.1) | collective-permute-done | bytes 294944 | tf_op jit(solution)/shard_map/ppermute | solution.py:249
  22.9 5.2 %collective-permute-done.2.refs_3_ = bf16[576,256]{1,0:T(8,128)(2,1)S(1)} collective-permute-done((bf16[576,256]{1,0:T(8,128)(2,1)S(1)}, bf16[576,256]{1,0:T(8,128)(2,1)S(1)}, u32[]{:S(2)}, u32[]{:S(2)}) %collective-permute-start.2) | collective-permute-done | bytes 294944 | tf_op jit(solution)/shard_map/ppermute | solution.py:249
  28.2 0.0 all-to-all-done.query
  28.2 0.0 slice-start
  28.2 0.0 copy-done.4
  28.2 0.0 copy-start.1
  28.2 0.0 slice-start.1
  28.2 1.6 %attention.1 = bf16[8,136,128]{2,1,0:T(8,128)(2,1)S(1)} custom-call(s32[4]{0:T(128)S(1)} %copy-done.4, bf16[8,144,128]{2,1,0:T(8,128)(2,1)S(1)} %all-to-all-done.query, bf16[576,256]{1,0:T(8,128)(2,1)S(1)} %get-tuple-element.9.refs_0_, bf16[576,256]{1,0:T(8,128)(2,1)S(1)} %collective-permute-done.refs_1_, ...), custom_call_target="tpu_custom_call" | custom-call | flops 6000000000 | bytes 3145728 | tf_op jit(solution)/shard_map/attention/pallas_call | solution.py:264
  29.8 16.6 %all_to_all.15.received = bf16[8,136,128]{2,1,0:T(8,128)(2,1)S(1)} all-to-all(bf16[8,136,128]{2,1,0:T(8,128)(2,1)S(1)} %attention.1), channel_id=1, replica_groups=mesh['seq'=8,'grp'=4] {'seq'}, dimensions={0} | all-to-all | bytes 557056 | tf_op jit(solution)/shard_map/all_to_all | solution.py:276
  46.5 0.0 copy-done.1
  46.5 1.0 %merge.1 = bf16[32,128]{1,0:T(8,128)(2,1)S(1)} custom-call(bf16[8,136,128]{2,1,0:T(8,128)(2,1)S(1)} %all_to_all.15.received, bf16[16,512,128]{2,1,0:T(8,128)(2,1)S(1)} %copy-done.1), custom_call_target="tpu_custom_call" | custom-call | tf_op jit(solution)/shard_map/merge/pallas_call | solution.py:277
  47.5 5.2 %all_gather.3.values = bf16[128,128]{1,0:T(8,128)(2,1)S(1)} all-gather(bf16[32,128]{1,0:T(8,128)(2,1)S(1)} %merge.1), channel_id=1, replica_groups=mesh['seq'=8,'grp'=4] {'grp'}, dimensions={0}, use_global_device_ids=true | all-gather | bytes 40960 | tf_op jit(solution)/shard_map/all_gather | solution.py:286
  52.6 0.0 slice-done
  52.6 0.0 slice-done.1
  52.6 1.1 %project.1 = bf16[8,8,224]{2,1,0:T(8,128)(2,1)S(1)} custom-call(bf16[128,128]{1,0:T(8,128)(2,1)S(1)} %all_gather.3.values, bf16[2048,1792]{1,0:T(8,128)(2,1)S(1)} %bitcast.4), custom_call_target="tpu_custom_call" | custom-call | tf_op jit(solution)/shard_map/project/pallas_call | solution.py:290
  53.8 9.3 %all_to_all.16 = bf16[8,8,224]{2,1,0:T(8,128)(2,1)S(1)} all-to-all(bf16[8,8,224]{2,1,0:T(8,128)(2,1)S(1)} %project.1), channel_id=1, replica_groups=mesh['seq'=8,'grp'=4] {'seq'}, dimensions={0} | all-to-all | bytes 57344 | tf_op jit(solution)/shard_map/all_to_all | solution.py:299
  63.1 0.6 reshape.11
  (2 shorter events, 0.0 us)
Async XLA Ops:
  0.0 1.6 %copy-start = (bf16[16,128,512]{2,1,0:T(8,128)(2,1)S(1)}, bf16[16,128,512]{2,1,0:T(8,128)(2,1)}, u32[]{:S(2)}) copy-start(bf16[16,128,512]{2,1,0:T(8,128)(2,1)} %weight.3) | copy-start | bytes 6291460
  1.6 0.8 %copy-start.2 = (bf16[4,2,16,128]{3,2,1,0:T(8,128)(2,1)S(1)}, bf16[4,2,16,128]{3,2,1,0:T(8,128)(2,1)}, u32[]{:S(2)}) copy-start(bf16[4,2,16,128]{3,2,1,0:T(8,128)(2,1)} %param.7) | copy-start | bytes 98308
  2.4 0.8 %copy-start.3 = (bf16[4,2,16,64]{3,2,1,0:T(8,128)(2,1)S(1)}, bf16[4,2,16,64]{3,2,1,0:T(8,128)(2,1)}, u32[]{:S(2)}) copy-start(bf16[4,2,16,64]{3,2,1,0:T(8,128)(2,1)} %param.8) | copy-start | bytes 49156
  4.3 23.9 %all-to-all-start = ((bf16[8,144,128]{2,1,0:T(8,128)(2,1)}), bf16[8,144,128]{2,1,0:T(8,128)(2,1)S(1)}, u32[]{:S(2)}, u32[]{:S(2)}) async-start(bf16[8,144,128]{2,1,0:T(8,128)(2,1)} %absorb.1), calls=%async_computation | async-start | bytes 589824 | tf_op jit(solution)/shard_map/all_to_all | solution.py:262
  11.6 16.6 %copy-start.4 = (s32[4]{0:T(128)S(1)}, s32[4]{0:T(128)}, u32[]{:S(2)}) copy-start(s32[4]{0:T(128)} %lengths.1) | copy-start | bytes 52
  12.9 1.9 %collective-permute-start = (bf16[576,256]{1,0:T(8,128)(2,1)S(1)}, bf16[576,256]{1,0:T(8,128)(2,1)S(1)}, u32[]{:S(2)}, u32[]{:S(2)}) collective-permute-start(bf16[576,256]{1,0:T(8,128)(2,1)S(1)} %get-tuple-element.10), channel_id=1, source_target_pairs={{0,1},{1,0},{2,3},{3,2},{4,5},{5,4},{6,7},{7,6},{8,9},{9,8},{10,11... | collective-permute-start | bytes 884744 | tf_op jit(solution)/shard_map/ppermute | solution.py:249
  13.0 9.9 %collective-permute-start.1 = (bf16[576,256]{1,0:T(8,128)(2,1)S(1)}, bf16[576,256]{1,0:T(8,128)(2,1)S(1)}, u32[]{:S(2)}, u32[]{:S(2)}) collective-permute-start(bf16[576,256]{1,0:T(8,128)(2,1)S(1)} %get-tuple-element.11), channel_id=1, source_target_pairs={{0,2},{1,3},{2,0},{3,1},{4,6},{5,7},{6,4},{7,5},{8,10},{9,11},{10,... | collective-permute-start | bytes 884744 | tf_op jit(solution)/shard_map/ppermute | solution.py:249
  14.5 13.6 %collective-permute-start.2 = (bf16[576,256]{1,0:T(8,128)(2,1)S(1)}, bf16[576,256]{1,0:T(8,128)(2,1)S(1)}, u32[]{:S(2)}, u32[]{:S(2)}) collective-permute-start(bf16[576,256]{1,0:T(8,128)(2,1)S(1)} %get-tuple-element.12), channel_id=1, source_target_pairs={{0,3},{1,2},{2,1},{3,0},{4,7},{5,6},{6,5},{7,4},{8,11},{9,10},{10,... | collective-permute-start | bytes 884744 | tf_op jit(solution)/shard_map/ppermute | solution.py:249
  28.2 24.5 %slice-start = ((s8[7340032]{0:T(1024)(128)(4,1)}), s8[4194304]{0:T(1024)(128)(4,1)S(1)}, s32[]{:S(2)}) async-start(s8[7340032]{0:T(1024)(128)(4,1)} %bitcast.3), calls=%async_computation.3 | async-start | bytes 8388608
  28.2 18.3 %copy-start.1 = (bf16[16,512,128]{2,1,0:T(8,128)(2,1)S(1)}, bf16[16,512,128]{2,1,0:T(8,128)(2,1)}, u32[]{:S(2)}) copy-start(bf16[16,512,128]{2,1,0:T(8,128)(2,1)} %weight.4) | copy-start | bytes 6291460
  28.2 24.4 %slice-start.1 = ((s8[7340032]{0:T(1024)(128)(4,1)}), s8[3145728]{0:T(1024)(128)(4,1)S(1)}, s32[]{:S(2)}) async-start(s8[7340032]{0:T(1024)(128)(4,1)} %bitcast.3), calls=%async_computation.4 | async-start | bytes 6291456

commit v4 on v3

--- a/solution.py
+++ b/solution.py
@@ -32,6 +32,7 @@
         and drafts * rope == LANES
         and LANES % rows == 0
         and n_seq * rows % LANES == 0
+        and n_seq <= LANES
     )
 
 
@@ -45,10 +46,19 @@
     parts.append(
         jnp.concatenate([jnp.where(owner == t, tail, zero) for t in range(drafts)], axis=1)
     )
-    return jnp.concatenate([part.reshape(n_seq * rows, lanes) for part in parts], axis=-1)
-
-
-def attention_kernel(factor, latent, heads, drafts, partners, packed, lengths, query, *refs):
+    parts = [part.reshape(n_seq * rows, lanes) for part in parts]
+    return jnp.concatenate(parts[:-1], axis=-1), parts[-1]
+
+
+def attention_kernel(factor, latent, heads, drafts, partners, packed, apart, lengths, *refs):
+    if apart:
+        query = refs[-1]
+        seq = lax.axis_index("seq")
+        for k in range(apart):
+            query[seq ^ k] = refs[k][0]
+        refs = refs[apart:-1]
+    else:
+        query, refs = refs[0], refs[1:]
     caches, out = refs[:-1], refs[-1]
     rows = query.shape[0] * drafts * heads if packed else query.shape[0]
     width = caches[0].shape[1]
@@ -58,10 +68,13 @@
     queries = unpack_queries(query, latent, heads, drafts) if packed else query[...]
     scores = []
     for j, cache in enumerate(caches):
-        keys = cache[...]
         if packed:
-            keys = jnp.concatenate([keys] + [cache[latent:, :]] * (drafts - 1), axis=0)
-        raw = jnp.dot(queries, keys, preferred_element_type=jnp.float32) * factor
+            tail = jnp.concatenate([cache[latent:, :]] * drafts, axis=0)
+            raw = jnp.dot(queries[0], cache[:latent, :], preferred_element_type=jnp.float32)
+            raw = raw + jnp.dot(queries[1], tail, preferred_element_type=jnp.float32)
+        else:
+            raw = jnp.dot(queries, cache[...], preferred_element_type=jnp.float32)
+        raw = raw * factor
         offset = (seq * len(caches) + partners[j](grp)) * width
         places = offset + lax.broadcasted_iota(jnp.int32, (rows, width), 1)
         scores.append(jnp.where(places < limit, raw, NEGATIVE))
@@ -79,15 +92,20 @@
         )
     result = (summed / total).astype(jnp.bfloat16)
     lane = lax.broadcasted_iota(jnp.int32, (rows, LANES), 1)
-    stats = jnp.zeros((rows, LANES), jnp.float32)
-    for i, piece in enumerate(split3(top) + split3(total)):
-        stats = jnp.where(lane == i, piece, stats)
     if not packed:
+        stats = jnp.zeros((rows, LANES), jnp.float32)
+        for i, piece in enumerate(split3(top) + split3(total)):
+            stats = jnp.where(lane == i, piece, stats)
         out[:, :latent] = result
         out[:, latent:] = stats.astype(jnp.bfloat16)
         return
     block = drafts * heads
-    by_stat = stats.T[:STATS].astype(jnp.bfloat16)
+    turned = jnp.where(lane == 0, top, total).T[:STATS]
+    place = lax.broadcasted_iota(jnp.int32, (STATS, rows), 0)
+    by_stat = jnp.zeros((STATS, rows), jnp.float32)
+    for i, piece in enumerate(split3(turned[0:1]) + split3(turned[1:2])):
+        by_stat = jnp.where(place == i, piece, by_stat)
+    by_stat = by_stat.astype(jnp.bfloat16)
     for i in range(rows // block):
         for c in chunks(latent):
             lanes = slice(c * LANES, (c + 1) * LANES)
@@ -146,33 +164,33 @@
     if packed:
         turned = scratch[0]
         first = len(chunks(latent)) * rows
-        stats = received[:, first:, :].astype(jnp.float32).reshape(sources * STATS, LANES)
-        turned[...] = stats.T
+        stats = received[:, first:, :].astype(jnp.float32)
+    else:
+        block = received[...]
+        stats = block[:, :, latent:].astype(jnp.float32)
+
+    def stat(i):
+        return stats[:, i, :] if packed else stats[:, :, i : i + 1]
+
+    top = (stat(0) + stat(1)) + stat(2)
+    shares = ((stat(3) + stat(4)) + stat(5)) * jnp.exp(top - jnp.max(top, axis=0, keepdims=True))
+    shares = shares / jnp.sum(shares, axis=0, keepdims=True)
+    if packed:
+        turned[...] = jnp.concatenate([shares, jnp.zeros((LANES - sources, LANES), jnp.float32)]).T
         start = lax.axis_index("seq") * rows % LANES
         own = turned[pl.ds(pl.multiple_of(start, rows), rows), :]
-        columns = [[own[:, j * STATS + i : j * STATS + i + 1] for i in range(6)] for j in range(sources)]
+        shares = [own[:, j : j + 1] for j in range(sources)]
         parts = [
             [received[j, c * rows : (c + 1) * rows, :] for j in range(sources)]
             for c in chunks(latent)
         ]
     else:
-        block = received[...]
-        stats = block[:, :, latent:].astype(jnp.float32)
-        columns = [[stats[j, :, i : i + 1] for i in range(6)] for j in range(sources)]
         parts = [[block[j, :, :latent] for j in range(sources)]]
-    tops = [(column[0] + column[1]) + column[2] for column in columns]
-    peak = functools.reduce(jnp.maximum, tops)
-    shares = [
-        ((column[3] + column[4]) + column[5]) * jnp.exp(top - peak)
-        for column, top in zip(columns, tops)
-    ]
-    summed = functools.reduce(jnp.add, shares)
     merged = jnp.concatenate(
         [
             functools.reduce(
-                jnp.add, [share * piece.astype(jnp.float32) for share, piece in zip(shares, part)]
+                jnp.add, [shares[j] * piece.astype(jnp.float32) for j, piece in enumerate(part)]
             )
-            / summed
             for part in parts
         ],
         axis=-1,
@@ -220,6 +238,7 @@
     rows = drafts * heads
     assert requests == n_grp
     packed = packs(n_seq, drafts, heads, latent, rope)
+    apart = n_seq if packed and n_seq in (2, 4, 8) else 0
     asked = (rows * len(chunks(latent)) + heads, LANES) if packed else (rows, width)
     given = (rows * len(chunks(latent)) + STATS, LANES) if packed else (rows, latent + LANES)
 
@@ -249,7 +268,7 @@
         caches.append(piece if k in kept else lax.ppermute(piece, "grp", routes[k]))
     queries = pl.pallas_call(
         functools.partial(absorb_kernel, drafts, packed),
-        out_shape=jax.ShapeDtypeStruct((n_seq,) + asked, jnp.bfloat16),
+        out_shape=jax.ShapeDtypeStruct((1 if apart else n_seq,) + asked, jnp.bfloat16),
         in_specs=whole(3),
         out_specs=whole(1)[0],
         compiler_params=kernel_params(8),
@@ -259,19 +278,27 @@
         query_rope.reshape(requests, rows, rope),
         key_weight,
     )
-    queries = lax.all_to_all(queries, "seq", 0, 0, tiled=True)
+    if apart:
+        arrived = {0: queries}
+        for k in range(1, n_seq):
+            arrived[k] = lax.ppermute(queries, "seq", [(i, i ^ k) for i in range(n_seq)])
+        queries = [arrived[k] for k in range(n_seq)]
+    else:
+        queries = lax.all_to_all(queries, "seq", 0, 0, tiled=True)
+        queries = [queries if packed else queries.reshape(n_seq * rows, width)]
 
     partial = pl.pallas_call(
-        functools.partial(attention_kernel, factor, latent, heads, drafts, partners, packed),
+        functools.partial(attention_kernel, factor, latent, heads, drafts, partners, packed, apart),
         out_shape=jax.ShapeDtypeStruct(
             (n_seq,) + given if packed else (n_seq * rows,) + given[1:], jnp.bfloat16
         ),
-        in_specs=[smem] + whole(1 + n_grp),
+        in_specs=[smem] + whole(len(queries) + n_grp),
         out_specs=whole(1)[0],
+        scratch_shapes=[pltpu.VMEM((n_seq,) + asked, jnp.bfloat16)] if apart else [],
         compiler_params=kernel_params(12),
         cost_estimate=pl.CostEstimate(flops=6 * 10**9, transcendentals=0, bytes_accessed=3 << 20),
         name="attention",
-    )(lengths, queries if packed else queries.reshape(n_seq * rows, width), *caches)
+    )(lengths, *queries, *caches)
 
     received = lax.all_to_all(partial.reshape((n_seq,) + given), "seq", 0, 0, tiled=True)
     values = pl.pallas_call(
@@ -279,7 +306,7 @@
         out_shape=jax.ShapeDtypeStruct((rows, value_weight.shape[2]), jnp.bfloat16),
         in_specs=whole(2),
         out_specs=whole(1)[0],
-        scratch_shapes=[pltpu.VMEM((LANES, n_seq * STATS), jnp.float32)] * packed,
+        scratch_shapes=[pltpu.VMEM((LANES, LANES), jnp.float32)] * packed,
         compiler_params=kernel_params(8),
         name="merge",
     )(received, value_weight)

time: 64.1 us -> 60.3 us (0.941)
  starting transfers between devices: 9.23 us -> 16.1 us
  waiting for transfers between devices: 13.3 us -> 8.7 us
  local copies, waits for them, and re-layouts: 3.73 us -> 0.64 us
  blocking collectives: 31.1 us -> 29.3 us
  Pallas kernels: 6.19 us -> 5.27 us
    ppermute x3, waiting for transfers between devices: 13.3 us -> 0.01 us  [shards(): caches.append(piece if k in kept else lax.ppermute(piece, 'grp', routes[k]))]
    ppermute x0 -> x7, starting transfers between devices: none -> 12.9 us  [shards(): lax.ppermute(queries, 'seq', [(i, i ^ k) for i in range(n_seq)])]
    ppermute x0 -> x7, waiting for transfers between devices: none -> 8.69 us  [shards(): lax.ppermute(queries, 'seq', [(i, i ^ k) for i in range(n_seq)])]
    all_to_all x1 -> x0, starting transfers between devices: 7.31 us -> none  [shards(): queries = lax.all_to_all(queries, 'seq', 0, 0, tiled=True)]
    unnamed x14, local copies, waits for them, and re-layouts: 3.12 us -> 0.04 us
    all_to_all x1, blocking collectives: 16.6 us -> 15 us  [shards(): lax.all_to_all(partial.reshape((n_seq,) + given), 'seq', 0, 0, tiled=True)]
    ppermute x3, starting transfers between devices: 1.92 us -> 3.16 us  [shards(): caches.append(piece if k in kept else lax.ppermute(piece, 'grp', routes[k]))]
    pallas_call x1, Pallas kernels: 1.2 us -> 0.45 us  [shards(): pl.pallas_call(functools.partial(absorb_kernel, drafts, packed), out_shap...]
  transfers between devices with their start and end apart: 4 -> 10, of which waited for: 2 -> 6; matrix products, arithmetic and copies ran while one was open for 0% -> 0% of each run, Pallas kernels for 2% -> 1%
where the time goes in v4:
time: 60.3 us; the launch traced here: 60.1 us
  blocking collectives  29.3 us (49%)
  starting transfers between devices  16.1 us (27%)
  waiting for transfers between devices  8.7 us (14%)
  Pallas kernels  5.27 us (9%)
  local copies, waits for them, and re-layouts  0.64 us (1%)
    all_to_all x1, blocking collectives, shards(): lax.all_to_all(partial.reshape((n_seq,) + given), 'seq', 0, 0, tiled=True)  15 us
    ppermute x7, starting transfers between devices, shards(): lax.ppermute(queries, 'seq', [(i, i ^ k) for i in range(n_seq)])  12.9 us
    all_to_all x1, blocking collectives, shards(): terms = lax.all_to_all(terms, 'seq', 0, 0, tiled=True)  9.09 us
    ppermute x7, waiting for transfers between devices, shards(): lax.ppermute(queries, 'seq', [(i, i ^ k) for i in range(n_seq)])  8.69 us
    all_gather x1, blocking collectives, shards(): values = lax.all_gather(values, 'grp', axis=0, tiled=True)  5.19 us
    ppermute x3, starting transfers between devices, shards(): caches.append(piece if k in kept else lax.ppermute(piece, 'grp', routes[k]))  3.16 us
    pallas_call x1, Pallas kernels, shards(): pl.pallas_call(functools.partial(attention_kernel, factor, latent, heads,...  1.62 us
    pallas_call x1, Pallas kernels, shards(): pl.pallas_call(functools.partial(pick_kernel, partners), out_shape=[jax.S...  1.41 us
  transfers between devices with their start and end apart: 10, of which 6 were waited for; matrix products, arithmetic and copies ran while one was open for 0% of the time, Pallas kernels for 1%

profile of v4, /device:TPU:0, one launch (start us, length us, event | category | flops | bytes accessed | tf_op | source)
XLA Modules:
  0.0 60.1 jit_solution(7484538236897149543)
XLA Ops:
  0.0 0.0 copy-start.1
  0.0 0.0 copy-start.2
  0.0 0.0 copy-start.3
  0.0 1.4 %pick.1 = (bf16[576,256]{1,0:T(8,128)(2,1)S(1)}, bf16[576,256]{1,0:T(8,128)(2,1)S(1)}, bf16[576,256]{1,0:T(8,128)(2,1)S(1)}, bf16[576,256]{1,0:T(8,128)(2,1)S(1)}) custom-call(bf16[4,576,256]{2,1,0:T(8,128)(2,1)} %bitcast.7), custom_call_target="tpu_custom_call" | custom-call | flops 3000000000 | bytes 2097152 | tf_op jit(solution)/shard_map/pick/pallas_call | solution.py:256
  1.4 0.0 copy-start.4
  1.4 0.6 collective-permute-start.7
  2.0 2.6 %collective-permute-start.8 = (bf16[576,256]{1,0:T(8,128)(2,1)S(1)}, bf16[576,256]{1,0:T(8,128)(2,1)S(1)}, u32[]{:S(2)}, u32[]{:S(2)}) collective-permute-start(bf16[576,256]{1,0:T(8,128)(2,1)S(1)} %get-tuple-element.11), channel_id=1, source_target_pairs={{0,2},{1,3},{2,0},{3,1},{4,6},{5,7},{6,4},{7,5},{8,10},{9,11},{10,... | collective-permute-start | bytes 884744 | tf_op jit(solution)/shard_map/ppermute | solution.py:268
  4.6 0.0 collective-permute-start.9
  4.6 0.0 copy-done.1
  4.6 0.0 copy-done.2
  4.6 0.0 copy-done.3
  4.6 0.5 absorb.1.refs_0_
  5.1 4.8 %collective-permute-start.6 = (bf16[1,144,128]{2,1,0:T(8,128)(2,1)S(1)}, bf16[1,144,128]{2,1,0:T(8,128)(2,1)S(1)}, u32[]{:S(2)}, u32[]{:S(2)}) collective-permute-start(bf16[1,144,128]{2,1,0:T(8,128)(2,1)S(1)} %absorb.1.refs_0_), channel_id=1, source_target_pairs={{0,28},{4,24},{8,20},{12,16},{16,12},{20,8},{24,4},{28,0},{1,29},{... | collective-permute-start | bytes 110600 | tf_op jit(solution)/shard_map/ppermute | solution.py:284
  9.9 0.2 collective-permute-start.5
  10.1 1.9 %collective-permute-done.6.refs_7_ = bf16[1,144,128]{2,1,0:T(8,128)(2,1)S(1)} collective-permute-done((bf16[1,144,128]{2,1,0:T(8,128)(2,1)S(1)}, bf16[1,144,128]{2,1,0:T(8,128)(2,1)S(1)}, u32[]{:S(2)}, u32[]{:S(2)}) %collective-permute-start.6) | collective-permute-done | bytes 36896 | tf_op jit(solution)/shard_map/ppermute | solution.py:284
  12.0 1.9 %collective-permute-start.4 = (bf16[1,144,128]{2,1,0:T(8,128)(2,1)S(1)}, bf16[1,144,128]{2,1,0:T(8,128)(2,1)S(1)}, u32[]{:S(2)}, u32[]{:S(2)}) collective-permute-start(bf16[1,144,128]{2,1,0:T(8,128)(2,1)S(1)} %absorb.1.refs_0_), channel_id=1, source_target_pairs={{0,20},{4,16},{8,28},{12,24},{16,4},{20,0},{24,12},{28,8},{1,21},{... | collective-permute-start | bytes 110600 | tf_op jit(solution)/shard_map/ppermute | solution.py:284
  13.9 1.7 %collective-permute-done.5.refs_6_ = bf16[1,144,128]{2,1,0:T(8,128)(2,1)S(1)} collective-permute-done((bf16[1,144,128]{2,1,0:T(8,128)(2,1)S(1)}, bf16[1,144,128]{2,1,0:T(8,128)(2,1)S(1)}, u32[]{:S(2)}, u32[]{:S(2)}) %collective-permute-start.5) | collective-permute-done | bytes 36896 | tf_op jit(solution)/shard_map/ppermute | solution.py:284
  15.6 0.2 collective-permute-start.3
  15.9 1.9 %collective-permute-done.4.refs_5_ = bf16[1,144,128]{2,1,0:T(8,128)(2,1)S(1)} collective-permute-done((bf16[1,144,128]{2,1,0:T(8,128)(2,1)S(1)}, bf16[1,144,128]{2,1,0:T(8,128)(2,1)S(1)}, u32[]{:S(2)}, u32[]{:S(2)}) %collective-permute-start.4) | collective-permute-done | bytes 36896 | tf_op jit(solution)/shard_map/ppermute | solution.py:284
  17.7 1.7 %collective-permute-start.2 = (bf16[1,144,128]{2,1,0:T(8,128)(2,1)S(1)}, bf16[1,144,128]{2,1,0:T(8,128)(2,1)S(1)}, u32[]{:S(2)}, u32[]{:S(2)}) collective-permute-start(bf16[1,144,128]{2,1,0:T(8,128)(2,1)S(1)} %absorb.1.refs_0_), channel_id=1, source_target_pairs={{0,12},{4,8},{8,4},{12,0},{16,28},{20,24},{24,20},{28,16},{1,13},{... | collective-permute-start | bytes 110600 | tf_op jit(solution)/shard_map/ppermute | solution.py:284
  19.5 1.1 %collective-permute-done.3.refs_4_ = bf16[1,144,128]{2,1,0:T(8,128)(2,1)S(1)} collective-permute-done((bf16[1,144,128]{2,1,0:T(8,128)(2,1)S(1)}, bf16[1,144,128]{2,1,0:T(8,128)(2,1)S(1)}, u32[]{:S(2)}, u32[]{:S(2)}) %collective-permute-start.3) | collective-permute-done | bytes 36896 | tf_op jit(solution)/shard_map/ppermute | solution.py:284
  20.5 1.9 %collective-permute-start.1 = (bf16[1,144,128]{2,1,0:T(8,128)(2,1)S(1)}, bf16[1,144,128]{2,1,0:T(8,128)(2,1)S(1)}, u32[]{:S(2)}, u32[]{:S(2)}) collective-permute-start(bf16[1,144,128]{2,1,0:T(8,128)(2,1)S(1)} %absorb.1.refs_0_), channel_id=1, source_target_pairs={{0,8},{4,12},{8,0},{12,4},{16,24},{20,28},{24,16},{28,20},{1,9},{5... | collective-permute-start | bytes 110600 | tf_op jit(solution)/shard_map/ppermute | solution.py:284
  22.4 0.2 collective-permute-done.2.refs_3_
  22.6 2.1 %collective-permute-start = (bf16[1,144,128]{2,1,0:T(8,128)(2,1)S(1)}, bf16[1,144,128]{2,1,0:T(8,128)(2,1)S(1)}, u32[]{:S(2)}, u32[]{:S(2)}) collective-permute-start(bf16[1,144,128]{2,1,0:T(8,128)(2,1)S(1)} %absorb.1.refs_0_), channel_id=1, source_target_pairs={{0,4},{4,0},{8,12},{12,8},{16,20},{20,16},{24,28},{28,24},{1,5},{5... | collective-permute-start | bytes 110600 | tf_op jit(solution)/shard_map/ppermute | solution.py:284
  24.8 0.0 collective-permute-done.1.refs_2_
  24.8 1.9 %collective-permute-done.refs_1_ = bf16[1,144,128]{2,1,0:T(8,128)(2,1)S(1)} collective-permute-done((bf16[1,144,128]{2,1,0:T(8,128)(2,1)S(1)}, bf16[1,144,128]{2,1,0:T(8,128)(2,1)S(1)}, u32[]{:S(2)}, u32[]{:S(2)}) %collective-permute-start) | collective-permute-done | bytes 36896 | tf_op jit(solution)/shard_map/ppermute | solution.py:284
  26.7 0.0 collective-permute-done.7.refs_9_
  26.7 0.0 collective-permute-done.8.refs_10_
  26.7 0.0 collective-permute-done.9.refs_11_
  26.7 0.0 slice-start
  26.7 0.0 copy-done.4
  26.7 0.0 copy-start
  26.7 0.0 slice-start.1
  26.7 1.6 %attention.1 = bf16[8,136,128]{2,1,0:T(8,128)(2,1)S(1)} custom-call(s32[4]{0:T(128)S(1)} %copy-done.4, bf16[1,144,128]{2,1,0:T(8,128)(2,1)S(1)} %absorb.1.refs_0_, bf16[1,144,128]{2,1,0:T(8,128)(2,1)S(1)} %collective-permute-done.refs_1_, bf16[1,144,128]{2,1,0:T(8,128)(2,1)S(1)} %collective-permute-done.1.refs_2_, ...), custom_call_target="tpu_custom_call" | custom-call | flops 6000000000 | bytes 3145728 | tf_op jit(solution)/shard_map/attention/pallas_call | solution.py:290
  28.4 15.0 %all_to_all.10.received = bf16[8,136,128]{2,1,0:T(8,128)(2,1)S(1)} all-to-all(bf16[8,136,128]{2,1,0:T(8,128)(2,1)S(1)} %attention.1), channel_id=1, replica_groups=mesh['seq'=8,'grp'=4] {'seq'}, dimensions={0} | all-to-all | bytes 557056 | tf_op jit(solution)/shard_map/all_to_all | solution.py:303
  43.4 0.0 copy-done
  43.4 0.7 %merge.1 = bf16[32,128]{1,0:T(8,128)(2,1)S(1)} custom-call(bf16[8,136,128]{2,1,0:T(8,128)(2,1)S(1)} %all_to_all.10.received, bf16[16,512,128]{2,1,0:T(8,128)(2,1)S(1)} %copy-done), custom_call_target="tpu_custom_call" | custom-call | tf_op jit(solution)/shard_map/merge/pallas_call | solution.py:304
  44.1 5.2 %all_gather.3.values = bf16[128,128]{1,0:T(8,128)(2,1)S(1)} all-gather(bf16[32,128]{1,0:T(8,128)(2,1)S(1)} %merge.1), channel_id=1, replica_groups=mesh['seq'=8,'grp'=4] {'grp'}, dimensions={0}, use_global_device_ids=true | all-gather | bytes 40960 | tf_op jit(solution)/shard_map/all_gather | solution.py:313
  49.3 0.0 slice-done
  49.3 0.0 slice-done.1
  49.3 1.1 %project.1 = bf16[8,8,224]{2,1,0:T(8,128)(2,1)S(1)} custom-call(bf16[128,128]{1,0:T(8,128)(2,1)S(1)} %all_gather.3.values, bf16[2048,1792]{1,0:T(8,128)(2,1)S(1)} %bitcast.4), custom_call_target="tpu_custom_call" | custom-call | tf_op jit(solution)/shard_map/project/pallas_call | solution.py:317
  50.4 9.1 %all_to_all.11 = bf16[8,8,224]{2,1,0:T(8,128)(2,1)S(1)} all-to-all(bf16[8,8,224]{2,1,0:T(8,128)(2,1)S(1)} %project.1), channel_id=1, replica_groups=mesh['seq'=8,'grp'=4] {'seq'}, dimensions={0} | all-to-all | bytes 57344 | tf_op jit(solution)/shard_map/all_to_all | solution.py:326
  59.5 0.6 %reshape.11 = bf16[4,2,224]{2,1,0:T(2,128)(2,1)} reshape(bf16[8,224]{1,0:T(8,128)(2,1)S(1)} %reduce_sum.12) | data formatting | bytes 7168 | tf_op jit(solution)/shard_map/reshape | solution.py:328
  (2 shorter events, 0.0 us)
Async XLA Ops:
  0.0 4.6 %copy-start.1 = (bf16[16,128,512]{2,1,0:T(8,128)(2,1)S(1)}, bf16[16,128,512]{2,1,0:T(8,128)(2,1)}, u32[]{:S(2)}) copy-start(bf16[16,128,512]{2,1,0:T(8,128)(2,1)} %weight.3) | copy-start | bytes 6291460
  0.0 4.6 %copy-start.2 = (bf16[4,2,16,128]{3,2,1,0:T(8,128)(2,1)S(1)}, bf16[4,2,16,128]{3,2,1,0:T(8,128)(2,1)}, u32[]{:S(2)}) copy-start(bf16[4,2,16,128]{3,2,1,0:T(8,128)(2,1)} %param.7) | copy-start | bytes 98308
  0.0 4.6 %copy-start.3 = (bf16[4,2,16,64]{3,2,1,0:T(8,128)(2,1)S(1)}, bf16[4,2,16,64]{3,2,1,0:T(8,128)(2,1)}, u32[]{:S(2)}) copy-start(bf16[4,2,16,64]{3,2,1,0:T(8,128)(2,1)} %param.8) | copy-start | bytes 49156
  1.4 25.3 %copy-start.4 = (s32[4]{0:T(128)S(1)}, s32[4]{0:T(128)}, u32[]{:S(2)}) copy-start(s32[4]{0:T(128)} %lengths.1) | copy-start | bytes 52
  1.4 25.3 %collective-permute-start.7 = (bf16[576,256]{1,0:T(8,128)(2,1)S(1)}, bf16[576,256]{1,0:T(8,128)(2,1)S(1)}, u32[]{:S(2)}, u32[]{:S(2)}) collective-permute-start(bf16[576,256]{1,0:T(8,128)(2,1)S(1)} %get-tuple-element.10), channel_id=1, source_target_pairs={{0,1},{1,0},{2,3},{3,2},{4,5},{5,4},{6,7},{7,6},{8,9},{9,8},{10,11... | collective-permute-start | bytes 884744 | tf_op jit(solution)/shard_map/ppermute | solution.py:268
  2.0 24.7 %collective-permute-start.8 = (bf16[576,256]{1,0:T(8,128)(2,1)S(1)}, bf16[576,256]{1,0:T(8,128)(2,1)S(1)}, u32[]{:S(2)}, u32[]{:S(2)}) collective-permute-start(bf16[576,256]{1,0:T(8,128)(2,1)S(1)} %get-tuple-element.11), channel_id=1, source_target_pairs={{0,2},{1,3},{2,0},{3,1},{4,6},{5,7},{6,4},{7,5},{8,10},{9,11},{10,... | collective-permute-start | bytes 884744 | tf_op jit(solution)/shard_map/ppermute | solution.py:268
  4.6 22.1 %collective-permute-start.9 = (bf16[576,256]{1,0:T(8,128)(2,1)S(1)}, bf16[576,256]{1,0:T(8,128)(2,1)S(1)}, u32[]{:S(2)}, u32[]{:S(2)}) collective-permute-start(bf16[576,256]{1,0:T(8,128)(2,1)S(1)} %get-tuple-element.12), channel_id=1, source_target_pairs={{0,3},{1,2},{2,1},{3,0},{4,7},{5,6},{6,5},{7,4},{8,11},{9,10},{10,... | collective-permute-start | bytes 884744 | tf_op jit(solution)/shard_map/ppermute | solution.py:268
  5.1 6.9 %collective-permute-start.6 = (bf16[1,144,128]{2,1,0:T(8,128)(2,1)S(1)}, bf16[1,144,128]{2,1,0:T(8,128)(2,1)S(1)}, u32[]{:S(2)}, u32[]{:S(2)}) collective-permute-start(bf16[1,144,128]{2,1,0:T(8,128)(2,1)S(1)} %absorb.1.refs_0_), channel_id=1, source_target_pairs={{0,28},{4,24},{8,20},{12,16},{16,12},{20,8},{24,4},{28,0},{1,29},{... | collective-permute-start | bytes 110600 | tf_op jit(solution)/shard_map/ppermute | solution.py:284
  9.9 5.8 %collective-permute-start.5 = (bf16[1,144,128]{2,1,0:T(8,128)(2,1)S(1)}, bf16[1,144,128]{2,1,0:T(8,128)(2,1)S(1)}, u32[]{:S(2)}, u32[]{:S(2)}) collective-permute-start(bf16[1,144,128]{2,1,0:T(8,128)(2,1)S(1)} %absorb.1.refs_0_), channel_id=1, source_target_pairs={{0,24},{4,28},{8,16},{12,20},{16,8},{20,12},{24,0},{28,4},{1,25},{... | collective-permute-start | bytes 110600 | tf_op jit(solution)/shard_map/ppermute | solution.py:284
  12.0 5.8 %collective-permute-start.4 = (bf16[1,144,128]{2,1,0:T(8,128)(2,1)S(1)}, bf16[1,144,128]{2,1,0:T(8,128)(2,1)S(1)}, u32[]{:S(2)}, u32[]{:S(2)}) collective-permute-start(bf16[1,144,128]{2,1,0:T(8,128)(2,1)S(1)} %absorb.1.refs_0_), channel_id=1, source_target_pairs={{0,20},{4,16},{8,28},{12,24},{16,4},{20,0},{24,12},{28,8},{1,21},{... | collective-permute-start | bytes 110600 | tf_op jit(solution)/shard_map/ppermute | solution.py:284
  15.6 4.9 %collective-permute-start.3 = (bf16[1,144,128]{2,1,0:T(8,128)(2,1)S(1)}, bf16[1,144,128]{2,1,0:T(8,128)(2,1)S(1)}, u32[]{:S(2)}, u32[]{:S(2)}) collective-permute-start(bf16[1,144,128]{2,1,0:T(8,128)(2,1)S(1)} %absorb.1.refs_0_), channel_id=1, source_target_pairs={{0,16},{4,20},{8,24},{12,28},{16,0},{20,4},{24,8},{28,12},{1,17},{... | collective-permute-start | bytes 110600 | tf_op jit(solution)/shard_map/ppermute | solution.py:284
  17.7 4.9 %collective-permute-start.2 = (bf16[1,144,128]{2,1,0:T(8,128)(2,1)S(1)}, bf16[1,144,128]{2,1,0:T(8,128)(2,1)S(1)}, u32[]{:S(2)}, u32[]{:S(2)}) collective-permute-start(bf16[1,144,128]{2,1,0:T(8,128)(2,1)S(1)} %absorb.1.refs_0_), channel_id=1, source_target_pairs={{0,12},{4,8},{8,4},{12,0},{16,28},{20,24},{24,20},{28,16},{1,13},{... | collective-permute-start | bytes 110600 | tf_op jit(solution)/shard_map/ppermute | solution.py:284
  20.5 4.2 %collective-permute-start.1 = (bf16[1,144,128]{2,1,0:T(8,128)(2,1)S(1)}, bf16[1,144,128]{2,1,0:T(8,128)(2,1)S(1)}, u32[]{:S(2)}, u32[]{:S(2)}) collective-permute-start(bf16[1,144,128]{2,1,0:T(8,128)(2,1)S(1)} %absorb.1.refs_0_), channel_id=1, source_target_pairs={{0,8},{4,12},{8,0},{12,4},{16,24},{20,28},{24,16},{28,20},{1,9},{5... | collective-permute-start | bytes 110600 | tf_op jit(solution)/shard_map/ppermute | solution.py:284
  22.6 4.1 %collective-permute-start = (bf16[1,144,128]{2,1,0:T(8,128)(2,1)S(1)}, bf16[1,144,128]{2,1,0:T(8,128)(2,1)S(1)}, u32[]{:S(2)}, u32[]{:S(2)}) collective-permute-start(bf16[1,144,128]{2,1,0:T(8,128)(2,1)S(1)} %absorb.1.refs_0_), channel_id=1, source_target_pairs={{0,4},{4,0},{8,12},{12,8},{16,20},{20,16},{24,28},{28,24},{1,5},{5... | collective-permute-start | bytes 110600 | tf_op jit(solution)/shard_map/ppermute | solution.py:284
  26.7 22.6 %slice-start = ((s8[7340032]{0:T(1024)(128)(4,1)}), s8[4194304]{0:T(1024)(128)(4,1)S(1)}, s32[]{:S(2)}) async-start(s8[7340032]{0:T(1024)(128)(4,1)} %bitcast.3), calls=%async_computation.2 | async-start | bytes 8388608
  26.7 16.7 %copy-start = (bf16[16,512,128]{2,1,0:T(8,128)(2,1)S(1)}, bf16[16,512,128]{2,1,0:T(8,128)(2,1)}, u32[]{:S(2)}) copy-start(bf16[16,512,128]{2,1,0:T(8,128)(2,1)} %weight.4) | copy-start | bytes 6291460
  26.7 22.5 %slice-start.1 = ((s8[7340032]{0:T(1024)(128)(4,1)}), s8[3145728]{0:T(1024)(128)(4,1)S(1)}, s32[]{:S(2)}) async-start(s8[7340032]{0:T(1024)(128)(4,1)} %bitcast.3), calls=%async_computation.3 | async-start | bytes 6291456
